TPU v7x, 128 devices: a whole 4x4x4 slice. The times are simulated.
128 devices in a mesh: dp: 4 (over x_hi, core), fsdp: 8 (over z, x_lo), tensor: 4 (over y).
Axes of the slice: x: 4 (x_hi: 2, x_lo: 2; x = x_hi * 2 + x_lo), y: 4, z: 4, core: 2. Of those that a mesh axis runs over, the one named last changes fastest.
Arguments:
- tokens: bfloat16 [32, 768, 8192], P(('dp', 'fsdp'), 'tensor'), may hold values from -6 to 6
- norm_gain: float32 [8192], replicated, may hold values from 0.85 to 4
- w_qkv: bfloat16 [8192, 5120], P(('dp', 'fsdp'), 'tensor'), may hold values from -0.3 to 0.3
- a_query: bfloat16 [8192, 16], replicated, may hold values from -0.0625 to 0.0625
- query_up_adapter: bfloat16 [16, 4096], P(None, 'tensor'), may hold values from -1.5 to 1.5
- a_value: bfloat16 [8192, 16], replicated, may hold values from -0.0625 to 0.0625
- value_up_adapter: bfloat16 [16, 512], P(None, 'tensor'), may hold values from -1.5 to 1.5
- out_grad: bfloat16 [32, 768, 4096], P(('dp', 'fsdp'), 'tensor'), may hold values from -6 to 6
Outputs:
- attn_out: bfloat16 [32, 768, 4096], P(('dp', 'fsdp'), 'tensor')
- grad_a_query: float32 [8192, 16], replicated
- grad_b_query: float32 [16, 4096], P(None, 'tensor')
- grad_a_value: float32 [8192, 16], replicated
- grad_b_value: float32 [16, 512], P(None, 'tensor')
All inputs are finite; a program needn't handle non-finite values.
Results may differ from a plain program's by a relative error of at most 0.015.
The roundings to bfloat16 on the way count: a program that leaves them out, or rounds other values in their place, can miss the bound.
Values may be sent and summed in bfloat16 or wider, within the bound.
A program may use at most 256 MiB of HBM per device.

v0:
```python
import math

import jax
import jax.numpy as jnp
from jax import lax
from jax.sharding import PartitionSpec as P

HD = 128
QUERY_PER_KV = 8


EPSILON = 1e-05
ADAPTER_SCALE = 2.0
ROPE_BASE = 500000.0


def from_everyone(array, axis):
    copies = jnp.broadcast_to(array, (lax.axis_size(axis), *array.shape))
    return lax.all_to_all(copies, axis, split_axis=0, concat_axis=0, tiled=True)


def joined_along(tiles, dim):
    lengths = list(tiles.shape[1:])
    lengths[dim] *= tiles.shape[0]
    return jnp.moveaxis(tiles, 0, dim).reshape(lengths)


def collect(array, axis, dim):
    tiles = from_everyone(array, axis)
    return joined_along(tiles, dim)


def of_everyone(array, axis):
    return from_everyone(array, axis).sum(axis=0)


def normalize(own_rows, norm_gain):
    widened = own_rows.astype(jnp.float32)
    mean_square = jnp.mean(widened * widened, axis=-1, keepdims=True)
    return (widened * lax.rsqrt(mean_square + EPSILON) * norm_gain).astype(jnp.bfloat16)


def rotary(heads_block):
    sequence_length = heads_block.shape[0]
    half_dim = heads_block.shape[-1] // 2
    positions = jnp.arange(sequence_length, dtype=jnp.float32)[:, None]
    inv_freq = ROPE_BASE ** (-jnp.arange(half_dim, dtype=jnp.float32) / half_dim)
    angles = positions * inv_freq
    cosine = jnp.cos(angles)[:, None, :]
    sine_table = jnp.sin(angles)[:, None, :]
    front_half = heads_block[..., :half_dim].astype(jnp.float32)
    back_half = heads_block[..., half_dim:].astype(jnp.float32)
    turned = jnp.concatenate(
        [
            front_half * cosine - back_half * sine_table,
            back_half * cosine + front_half * sine_table,
        ],
        -1,
    )
    return turned.astype(jnp.bfloat16)


def attend(query_rows, key_heads, value_rows):
    sequence_length = query_rows.shape[0]
    kv_heads = key_heads.shape[1] // HD
    rot_queries = rotary(query_rows.reshape(sequence_length, kv_heads * QUERY_PER_KV, HD))
    rot_keys = rotary(key_heads.reshape(sequence_length, kv_heads, HD))
    split_values = value_rows.reshape(sequence_length, kv_heads, HD)
    causal = jnp.arange(sequence_length)[:, None] >= jnp.arange(sequence_length)[None, :]

    def one_head(head_index):
        q_head = lax.dynamic_index_in_dim(rot_queries, head_index, 1, keepdims=False)
        k_head = lax.dynamic_index_in_dim(rot_keys, head_index // QUERY_PER_KV, 1, keepdims=False)
        v_head = lax.dynamic_index_in_dim(
            split_values, head_index // QUERY_PER_KV, 1, keepdims=False
        )
        scores = jnp.dot(q_head, k_head.T, preferred_element_type=jnp.float32) * (
            1.0 / math.sqrt(HD)
        )
        scores = jnp.where(causal, scores, -1e30)
        row_max = jnp.max(scores, axis=-1, keepdims=True)
        weights = jnp.exp(scores - row_max)
        probabilities = (weights / jnp.sum(weights, axis=-1, keepdims=True)).astype(jnp.bfloat16)
        return jnp.dot(probabilities, v_head, preferred_element_type=jnp.float32).astype(
            jnp.bfloat16
        )

    per_head = lax.map(one_head, jnp.arange(kv_heads * QUERY_PER_KV, dtype=jnp.int32))
    return jnp.transpose(per_head, (1, 0, 2)).reshape(sequence_length, kv_heads * QUERY_PER_KV * HD)


def local(tokens, norm_gain, w_qkv, a_query, query_up_adapter, a_value, value_up_adapter, out_grad):
    normed_input = normalize(tokens[0], norm_gain)
    gathered = collect(normed_input, "tensor", 0)
    sequence_length = gathered.shape[0]
    col_count = w_qkv.shape[1]
    weights = lax.all_gather(w_qkv, ("dp", "fsdp"), axis=0, tiled=True)
    projected = jnp.dot(gathered, weights, preferred_element_type=jnp.float32)
    narrow_rank_rows = a_query.shape[1]
    down_projected = jnp.dot(
        gathered, jnp.concatenate([a_query, a_value], 1), preferred_element_type=jnp.float32
    ).astype(jnp.bfloat16)
    kv_local = col_count // ((QUERY_PER_KV + 2) * HD)
    grouped_queries = projected.reshape(sequence_length, kv_local, QUERY_PER_KV + 2, HD)
    query_rows = (
        grouped_queries[:, :, :QUERY_PER_KV].reshape(sequence_length, -1)
        + ADAPTER_SCALE
        * jnp.dot(
            down_projected[:, :narrow_rank_rows],
            query_up_adapter,
            preferred_element_type=jnp.float32,
        )
    ).astype(jnp.bfloat16)
    key_heads = (
        grouped_queries[:, :, QUERY_PER_KV].reshape(sequence_length, -1).astype(jnp.bfloat16)
    )
    value_rows = (
        grouped_queries[:, :, QUERY_PER_KV + 1].reshape(sequence_length, -1)
        + ADAPTER_SCALE
        * jnp.dot(
            down_projected[:, narrow_rank_rows:],
            value_up_adapter,
            preferred_element_type=jnp.float32,
        )
    ).astype(jnp.bfloat16)
    grad_rows = lax.all_to_all(out_grad[0], "tensor", split_axis=1, concat_axis=0, tiled=True)
    attended, pullback = jax.vjp(attend, query_rows, key_heads, value_rows)
    query_gradient, grad_keys, value_gradient = pullback(grad_rows)
    out_rows = lax.all_to_all(attended, "tensor", split_axis=0, concat_axis=1, tiled=True)
    query_up_gradient = ADAPTER_SCALE * jnp.einsum(
        "fb,fd->bd",
        down_projected[:, :narrow_rank_rows],
        query_gradient,
        preferred_element_type=jnp.float32,
    )
    value_up_gradient = ADAPTER_SCALE * jnp.einsum(
        "fb,fd->bd",
        down_projected[:, narrow_rank_rows:],
        value_gradient,
        preferred_element_type=jnp.float32,
    )
    middle_gradient = jnp.concatenate(
        [
            jnp.dot(query_gradient, query_up_adapter.T, preferred_element_type=jnp.float32),
            jnp.dot(value_gradient, value_up_adapter.T, preferred_element_type=jnp.float32),
        ],
        1,
    )
    mid_summed = of_everyone(middle_gradient, "tensor").astype(jnp.bfloat16)
    down_gradient = ADAPTER_SCALE * jnp.einsum(
        "uh,ux->hx", gathered, mid_summed, preferred_element_type=jnp.float32
    )
    down_gradient, query_up_gradient, value_up_gradient = lax.psum(
        (down_gradient, query_up_gradient, value_up_gradient), ("dp", "fsdp")
    )
    return (
        out_rows[None],
        down_gradient[:, :narrow_rank_rows],
        query_up_gradient,
        down_gradient[:, narrow_rank_rows:],
        value_up_gradient,
    )


def solution(mesh):
    return jax.shard_map(
        local,
        mesh=mesh,
        in_specs=(
            P(("dp", "fsdp"), "tensor", None),
            P(),
            P(("dp", "fsdp"), "tensor"),
            P(),
            P(None, "tensor"),
            P(),
            P(None, "tensor"),
            P(("dp", "fsdp"), "tensor", None),
        ),
        out_specs=(
            P(("dp", "fsdp"), "tensor", None),
            P(),
            P(None, "tensor"),
            P(),
            P(None, "tensor"),
        ),
        check_vma=False,
    )
```

profile of v0, /device:TPU:1, one launch (start us, length us, event | category | flops | bytes accessed | tf_op | source)
XLA Modules:
  0.0 584.6 jit_solution(4451052558381677844)
XLA Ops:
  7.9 3.9 all_to_all.34
  11.8 3.2 copy.69
  15.0 5.0 all-to-all-start.2
  20.7 2.5 fusion.64
  23.2 16.9 %all-to-all-done.2 = bf16[192,4,1024]{2,0,1:T(8,128)(2,1)} async-done(((bf16[192,4,1024]{2,0,1:T(8,128)(2,1)}), bf16[192,4,1024]{2,0,1:T(8,128)(2,1)}, u32[]{:S(2)}, u32[]{:S(2)}) %all-to-all-start.2) | async-done | bytes 1572896 | tf_op jit(solution)/shard_map/all_to_all | solution.py:126
  40.1 8.0 %broadcast_in_dim.206 = bf16[4,192,8192]{2,1,0:T(8,128)(2,1)} broadcast(bf16[192,8192]{1,0:T(8,128)(2,1)} %fusion.64), dimensions={1,2} | broadcast | bytes 15728640 | tf_op jit(solution)/shard_map/broadcast_in_dim | solution.py:18
  48.1 6.6 %all-to-all-start = ((bf16[4,192,8192]{2,1,0:T(8,128)(2,1)}), bf16[4,192,8192]{2,1,0:T(8,128)(2,1)}, u32[]{:S(2)}, u32[]{:S(2)}) async-start(bf16[4,192,8192]{2,1,0:T(8,128)(2,1)} %broadcast_in_dim.206), calls=%async_computation | async-start | bytes 25165824 | tf_op jit(solution)/shard_map/all_to_all | solution.py:19
  56.4 1.9 copy.82
  59.7 132.0 %all-to-all-done = bf16[4,192,8192]{2,1,0:T(8,128)(2,1)} async-done(((bf16[4,192,8192]{2,1,0:T(8,128)(2,1)}), bf16[4,192,8192]{2,1,0:T(8,128)(2,1)}, u32[]{:S(2)}, u32[]{:S(2)}) %all-to-all-start) | async-done | bytes 12582944 | tf_op jit(solution)/shard_map/all_to_all | solution.py:19
  191.7 8.4 %convolution_convert_fusion.2 = bf16[768,32]{0,1:T(8,128)(2,1)S(1)} fusion(bf16[768,8192]{1,0:T(8,128)(2,1)} %bitcast.2, bf16[8192,16]{0,1:T(8,128)(2,1)S(1)} %copy-done.8, bf16[8192,16]{0,1:T(8,128)(2,1)S(1)} %copy-done.9), kind=kOutput, calls=%fused_computation.95 | convolution fusion | flops 403726336 | bytes 13156352 | tf_op jit(solution)/shard_map/dot_general | solution.py:100
  200.1 27.0 %copy.60 = bf16[1280,8192]{1,0:T(8,128)(2,1)} copy(bf16[1280,8192]{0,1:T(8,128)(2,1)} %bitcast.185) | data formatting | bytes 41943040 | tf_op jit(solution)/shard_map/dot_general | solution.py:98
  227.1 21.0 %convolution_bitcast_fusion = f32[768,1,10,128]{0,3,2,1:T(8,128)S(1)} fusion(bf16[768,8192,1]{1,0,2:T(8,128)(2,1)} %bitcast.3, bf16[10,128,8192]{2,1,0:T(8,128)(2,1)} %bitcast.186), kind=kOutput, calls=%fused_computation.78 | convolution fusion | flops 16106127360 | bytes 37486592 | tf_op jit(solution)/shard_map/dot_general | solution.py:98
  250.7 2.4 copy.61
  253.1 2.5 add_convert_fusion
  260.4 87.1 %while.52 = (s32[]{:T(128)}, bf16[8,768,128]{2,1,0:T(8,128)(2,1)}, s32[8]{0:T(128)S(1)}, bf16[8,128,768]{2,1,0:T(8,128)(2,1)}, f32[8,768,768]{1,2,0:T(8,128)}, /...) while((s32[]{:T(128)}, bf16[8,768,128]{2,1,0:T(8,128)(2,1)}, ...), condition=%wide.region_5.6_spmd.clone, body=%wide.region_1.5_spmd.clone.sunk | while | flops 310344960 | bytes 20494060 | solution.py:88
  264.7 2.5 fusion.125
  275.6 2.7 fusion.125
  286.6 2.5 fusion.125
  297.4 2.5 fusion.125
  308.3 2.6 fusion.125
  319.1 2.5 fusion.125
  329.9 2.6 fusion.125
  340.8 2.5 fusion.125
  347.6 93.7 %while.53 = (s32[]{:T(128)}, bf16[768,8,128]{0,2,1:T(8,128)(2,1)S(1)}, bf16[768,1,128]{2,0,1:T(8,128)(2,1)S(1)}, s32[8]{0:T(128)S(1)}, bf16[8,768,128]{2,1,0:T(8...) while((s32[]{:T(128)}, ...), condition=%wide.region_9.10_spmd.clone, body=%wide.region_6.9_spmd.clone.sunk | while | flops 464683776 | bytes 17364168 | solution.py:88
  347.7 2.4 fusion.130
  350.1 2.1 fusion.131
  353.6 3.0 fusion.132
  357.5 1.9 fusion.133
  359.4 2.4 fusion.130
  361.8 2.1 fusion.131
  365.3 3.0 fusion.132
  369.2 1.9 fusion.133
  371.1 2.4 fusion.130
  373.5 2.1 fusion.131
  377.0 3.0 fusion.132
  380.9 1.9 fusion.133
  382.8 2.4 fusion.130
  385.2 2.1 fusion.131
  388.7 3.0 fusion.132
  392.6 1.9 fusion.133
  394.5 2.4 fusion.130
  396.9 2.1 fusion.131
  400.5 3.0 fusion.132
  404.3 1.9 fusion.133
  406.2 2.4 fusion.130
  408.6 2.1 fusion.131
  412.2 3.0 fusion.132
  416.0 1.9 fusion.133
  417.9 2.4 fusion.130
  420.3 2.1 fusion.131
  423.9 3.0 fusion.132
  427.7 1.9 fusion.133
  429.7 2.4 fusion.130
  432.1 2.1 fusion.131
  435.6 3.0 fusion.132
  444.2 3.5 all-to-all-start.3
  448.9 5.0 all-to-all-done.3
  453.9 7.9 %convolution_multiply_fusion = f32[8192,32]{0,1:T(8,128)} fusion(bf16[768,8192]{1,0:T(8,128)(2,1)} %bitcast.2, bf16[768,32]{0,1:T(8,128)(2,1)S(1)} %reduce_sum.89), kind=kOutput, calls=%fused_computation.71 | convolution fusion | flops 402915328 | bytes 13680640 | tf_op jit(solution)/shard_map/uh,ux->hx/dot_general | solution.py:150
  462.9 2.1 all_to_all.31
  465.0 3.6 all-to-all-start.1
  468.7 64.0 %psum.23 = f32[16,128]{1,0:T(8,128)} all-reduce(f32[16,128]{1,0:T(8,128)S(1)} %convolution_multiply_fusion.3), channel_id=1, replica_groups=mesh['dp'=4,'fsdp'=8,'tensor'=4] {'dp','fsdp'}, use_global_device_ids=true, to_apply=%region_13.14 | all-reduce | flops 2048 | bytes 16384 | tf_op jit(solution)/shard_map/psum | solution.py:153
  532.7 38.6 %all-reduce.5.cloned.1.call-done = (f32[8192,32]{0,1:T(8,128)}, f32[16,1024]{1,0:T(8,128)}) async-done(((f32[8192,32]{0,1:T(8,128)}, f32[16,1024]{1,0:T(8,128)}), (f32[8192,32]{0,1:T(8,128)}, f32[16,1024]{1,0:T(8,128)})) %all-reduce.5.cloned.1.call-update) | async-done | bytes 1114128 | tf_op jit(solution)/shard_map/psum | solution.py:153
  571.3 2.2 fusion.94
  574.8 2.4 broadcast_in_dim.207
  (233 shorter events, 89.0 us)
Async XLA Ops:
  7.2 245.9 %copy-start = (bf16[16,1024]{1,0:T(8,128)(2,1)S(1)}, bf16[16,1024]{1,0:T(8,128)(2,1)}, u32[]{:S(2)}) copy-start(bf16[16,1024]{1,0:T(8,128)(2,1)} %param.16) | copy-start | bytes 98308
  7.2 192.9 %all-gather.2.cloned.1.call-start = ((), (), s32[]{:S(2)}) async-start(), calls=%async_computation.4 | async-start | bytes 21626880 | tf_op jit(solution)/shard_map/all_gather | solution.py:97
  11.8 8.2 %copy-start.1 = (bf16[1,192,8192]{2,1,0:T(8,128)(2,1)S(1)}, bf16[1,192,8192]{2,1,0:T(8,128)(2,1)}, u32[]{:S(2)}) copy-start(bf16[1,192,8192]{2,1,0:T(8,128)(2,1)} %param.12) | copy-start | bytes 9437188
  15.0 25.1 %all-to-all-start.2 = ((bf16[192,4,1024]{2,0,1:T(8,128)(2,1)}), bf16[192,4,1024]{2,0,1:T(8,128)(2,1)}, u32[]{:S(2)}, u32[]{:S(2)}) async-start(bf16[192,4,1024]{2,0,1:T(8,128)(2,1)} %copy.69), calls=%async_computation.2 | async-start | bytes 3145728 | tf_op jit(solution)/shard_map/all_to_all | solution.py:126
  20.0 0.8 copy-start.11
  48.1 143.6 %all-to-all-start = ((bf16[4,192,8192]{2,1,0:T(8,128)(2,1)}), bf16[4,192,8192]{2,1,0:T(8,128)(2,1)}, u32[]{:S(2)}, u32[]{:S(2)}) async-start(bf16[4,192,8192]{2,1,0:T(8,128)(2,1)} %broadcast_in_dim.206), calls=%async_computation | async-start | bytes 25165824 | tf_op jit(solution)/shard_map/all_to_all | solution.py:19
  58.3 133.4 %copy-start.8 = (bf16[8192,16]{0,1:T(8,128)(2,1)S(1)}, bf16[8192,16]{0,1:T(8,128)(2,1)}, u32[]{:S(2)}) copy-start(bf16[8192,16]{0,1:T(8,128)(2,1)} %param.17) | copy-start | bytes 786436
  58.3 133.4 %copy-start.9 = (bf16[8192,16]{0,1:T(8,128)(2,1)S(1)}, bf16[8192,16]{0,1:T(8,128)(2,1)}, u32[]{:S(2)}) copy-start(bf16[8192,16]{0,1:T(8,128)(2,1)} %param.15) | copy-start | bytes 786436
  248.1 1.9 copy-start.2
  255.6 0.9 copy-start.7
  255.6 1.8 copy-start.12
  260.4 87.2 %copy-start.6 = (bf16[768,1,128]{2,0,1:T(8,128)(2,1)S(1)}, bf16[768,1,128]{2,0,1:T(8,128)(2,1)}, u32[]{:S(2)}) copy-start(bf16[768,1,128]{2,0,1:T(8,128)(2,1)} %custom-call) | copy-start | bytes 589828
  441.3 0.9 copy-start.3
  441.3 1.0 copy-start.4
  444.2 9.7 %all-to-all-start.3 = ((f32[4,768,32]{1,2,0:T(8,128)}), f32[4,768,32]{1,2,0:T(8,128)S(1)}, u32[]{:S(2)}, u32[]{:S(2)}) async-start(f32[4,768,32]{1,2,0:T(8,128)} %broadcast_in_dim.210), calls=%async_computation.3 | async-start | bytes 786432 | tf_op jit(solution)/shard_map/all_to_all | solution.py:19
  447.7 123.6 %all-reduce.5.cloned.1.call-start = ((), (), s32[]{:S(2)}) async-start(), calls=%async_computation.5 | async-start | bytes 2228224 | tf_op jit(solution)/shard_map/psum | solution.py:153
  453.9 8.0 %copy-start.5 = (bf16[8,768,128]{2,1,0:T(8,128)(2,1)S(1)}, bf16[8,768,128]{2,1,0:T(8,128)(2,1)}, u32[]{:S(2)}) copy-start(bf16[8,768,128]{2,1,0:T(8,128)(2,1)} %get-tuple-element.648) | copy-start | bytes 4718596
  465.0 108.6 %all-to-all-start.1 = ((bf16[4,192,1024]{2,1,0:T(8,128)(2,1)}), bf16[4,192,1024]{2,1,0:T(8,128)(2,1)S(1)}, u32[]{:S(2)}, u32[]{:S(2)}) async-start(bf16[4,192,1024]{2,1,0:T(8,128)(2,1)} %all_to_all.31), calls=%async_computation.1 | async-start | bytes 3145728 | tf_op jit(solution)/shard_map/all_to_all | solution.py:129
  574.8 2.4 copy-start.10
Sparse Core Ops, SparseCore 0:
  9.7 125.2 all-gather.1
  462.0 109.2 all-reduce.4
where the time goes:
time: 587 us; the launch traced here: 585 us
  waiting for transfers between devices  193 us (33%)
  matrix products  115 us (20%)
  local copies, waits for them, and re-layouts  98.5 us (17%)
  blocking collectives  64 us (11%)
  other arithmetic  63.1 us (11%)
  starting transfers between devices  18.7 us (3%)
  loops' own time  17.5 us (3%)
  between operations  14.4 us (2%)
    all_to_all x2, waiting for transfers between devices, from_everyone(): return lax.all_to_all(copies, axis, split_axis=0, concat_axis=0, tiled=True)  137 us
    psum x1, blocking collectives, local(): lax.psum((down_gradient, query_up_gradient, value_up_gradient), ('dp', 'f...  64 us
    dot_general x24, matrix products, one_head(): jnp.dot(probabilities, v_head, preferred_element_type=jnp.float32)  43.6 us
    psum x1, waiting for transfers between devices, local(): lax.psum((down_gradient, query_up_gradient, value_up_gradient), ('dp', 'f...  38.6 us
    dynamic_update_slice x24, other arithmetic, attend(): lax.map(one_head, jnp.arange(kv_heads * QUERY_PER_KV, dtype=jnp.int32))  31.9 us
    dot_general x16, matrix products, one_head(): jnp.dot(q_head, k_head.T, preferred_element_type=jnp.float32)  28.8 us
    dot_general x1, local copies, waits for them, and re-layouts, local(): projected = jnp.dot(gathered, weights, preferred_element_type=jnp.float32)  27 us
    dot_general x1, matrix products, local(): projected = jnp.dot(gathered, weights, preferred_element_type=jnp.float32)  21 us
  transfers between devices with their start and end apart: 6, of which 4 were waited for; matrix products, arithmetic and copies ran while one was open for 6% of the time, Pallas kernels for 0%

commit v1 on v0

v1 whole, which is shorter than its diff:
```python
import functools
import math

import jax
import jax.numpy as jnp
from jax import lax
from jax.experimental import pallas as pl
from jax.experimental.pallas import tpu as pltpu
from jax.sharding import PartitionSpec as P

HD = 128
QUERY_PER_KV = 8
RANK = 16
QB = 256

EPSILON = 1e-05
ADAPTER_SCALE = 2.0
ROPE_BASE = 500000.0
SCORE_SCALE = 1.0 / math.sqrt(HD)
LOG2E = 1.4426950408889634
ALL = ("dp", "fsdp", "tensor")


def from_everyone(array, axis):
    copies = jnp.broadcast_to(array, (lax.axis_size(axis), *array.shape))
    return lax.all_to_all(copies, axis, split_axis=0, concat_axis=0, tiled=True)


def normalize(own_rows, norm_gain):
    widened = own_rows.astype(jnp.float32)
    mean_square = jnp.mean(widened * widened, axis=-1, keepdims=True)
    return (widened * lax.rsqrt(mean_square + EPSILON) * norm_gain).astype(jnp.bfloat16)


def rotary_tables(sequence_length):
    half_dim = HD // 2
    positions = jnp.arange(sequence_length, dtype=jnp.float32)[:, None]
    inv_freq = ROPE_BASE ** (-jnp.arange(half_dim, dtype=jnp.float32) / half_dim)
    angles = positions * inv_freq
    cosine = jnp.cos(angles)
    sine = jnp.sin(angles)
    return jnp.concatenate([cosine, cosine], 1), jnp.concatenate([-sine, sine], 1)


def dot_nt(a, b):
    return lax.dot_general(a, b, (((1,), (1,)), ((), ())), preferred_element_type=jnp.float32)


def dot_nn(a, b):
    return jnp.dot(a, b, preferred_element_type=jnp.float32)


def rotate(x, cos, sin):
    return x * cos + pltpu.roll(x, HD // 2, 1) * sin


def attention_kernel(
    seq,
    proj_ref,
    key_ref,
    value_ref,
    down_ref,
    down_t_ref,
    qup_ref,
    vup_ref,
    cos_ref,
    sin_ref,
    grad_ref,
    out_ref,
    gbq_ref,
    gbv_ref,
    mid_t_ref,
    k_scr,
    v_scr,
    dv_scr,
    q_scr,
    dq_scr,
    mid_scr,
):
    head = pl.program_id(0)
    blocks = seq // QB

    @pl.when(head == 0)
    def _():
        k_scr[...] = rotate(
            key_ref[...].astype(jnp.bfloat16).astype(jnp.float32), cos_ref[...], sin_ref[...]
        ).astype(jnp.bfloat16)
        v_scr[...] = (
            value_ref[...] + ADAPTER_SCALE * dot_nn(down_ref[:, RANK:], vup_ref[...])
        ).astype(jnp.bfloat16)
        dv_scr[...] = jnp.zeros_like(dv_scr)
        mid_scr[...] = jnp.zeros_like(mid_scr)

    queries = (proj_ref[...] + ADAPTER_SCALE * dot_nn(down_ref[:, :RANK], qup_ref[...])).astype(
        jnp.bfloat16
    )
    q_scr[...] = rotate(queries.astype(jnp.float32), cos_ref[...], sin_ref[...]).astype(
        jnp.bfloat16
    )
    row = lax.broadcasted_iota(jnp.int32, (QB, QB), 0)
    col = lax.broadcasted_iota(jnp.int32, (QB, QB), 1)
    causal = row >= col
    factor = SCORE_SCALE * LOG2E
    for i in range(blocks):
        rows = slice(i * QB, (i + 1) * QB)
        q = q_scr[rows, :]
        grad = grad_ref[rows, :]
        grad_t = grad.T
        scores = []
        for j in range(i + 1):
            s = dot_nt(q, k_scr[j * QB : (j + 1) * QB, :])
            if j == i:
                s = jnp.where(causal, s, -1e30)
            scores.append(s)
        top = functools.reduce(jnp.maximum, scores)
        top = jnp.max(top, axis=-1, keepdims=True) * factor
        weights = [jnp.exp2(s * factor - top) for s in scores]
        total = jnp.sum(functools.reduce(jnp.add, weights), axis=-1, keepdims=True)
        inverse = 1.0 / total
        probs = [w * inverse for w in weights]
        rounded = [p.astype(jnp.bfloat16) for p in probs]
        attended = functools.reduce(
            jnp.add, [dot_nn(rounded[j], v_scr[j * QB : (j + 1) * QB, :]) for j in range(i + 1)]
        )
        out_ref[rows, :] = attended.astype(jnp.bfloat16)
        prods = []
        for j in range(i + 1):
            keys = slice(j * QB, (j + 1) * QB)
            dp = dot_nt(grad, v_scr[keys, :])
            prods.append(probs[j] * dp)
            dv_scr[:, keys] += dot_nn(grad_t, rounded[j])
        inner = jnp.sum(functools.reduce(jnp.add, prods), axis=-1, keepdims=True)
        ds = [(prods[j] - probs[j] * inner).astype(jnp.bfloat16) for j in range(i + 1)]
        dq = functools.reduce(
            jnp.add, [dot_nn(ds[j], k_scr[j * QB : (j + 1) * QB, :]) for j in range(i + 1)]
        )
        dq = (dq * SCORE_SCALE).astype(jnp.bfloat16).astype(jnp.float32)
        dq_scr[rows, :] = rotate(dq, cos_ref[rows, :], -sin_ref[rows, :]).astype(jnp.bfloat16)
    dq = dq_scr[...]
    gbq_ref[...] = ADAPTER_SCALE * dot_nn(down_t_ref[:RANK, :], dq)
    mid_scr[...] += dot_nt(qup_ref[...], dq)

    @pl.when(head == QUERY_PER_KV - 1)
    def _():
        dv = dv_scr[...].T.astype(jnp.bfloat16)
        gbv_ref[...] = ADAPTER_SCALE * dot_nn(down_t_ref[RANK:, :], dv)
        mid_t_ref[:RANK, :] = mid_scr[...]
        mid_t_ref[RANK:, :] = dot_nt(vup_ref[...], dv)


def attention(projected, down, down_t, qup, vup, cos, sin, grad_rows):
    seq = projected.shape[0]
    heads = QUERY_PER_KV

    def whole(shape):
        return pl.BlockSpec(shape, lambda h: (0, 0))

    column = lambda h: (0, h)
    return pl.pallas_call(
        functools.partial(attention_kernel, seq),
        grid=(heads,),
        in_specs=[
            pl.BlockSpec((seq, HD), column),
            pl.BlockSpec((seq, HD), lambda h: (0, heads)),
            pl.BlockSpec((seq, HD), lambda h: (0, heads + 1)),
            whole((seq, 2 * RANK)),
            whole((2 * RANK, seq)),
            pl.BlockSpec((RANK, HD), column),
            whole((RANK, HD)),
            whole((seq, HD)),
            whole((seq, HD)),
            pl.BlockSpec((seq, HD), column),
        ],
        out_specs=[
            pl.BlockSpec((seq, HD), column),
            pl.BlockSpec((RANK, HD), column),
            whole((RANK, HD)),
            whole((2 * RANK, seq)),
        ],
        out_shape=[
            jax.ShapeDtypeStruct((seq, heads * HD), jnp.bfloat16),
            jax.ShapeDtypeStruct((RANK, heads * HD), jnp.float32),
            jax.ShapeDtypeStruct((RANK, HD), jnp.float32),
            jax.ShapeDtypeStruct((2 * RANK, seq), jnp.float32),
        ],
        scratch_shapes=[
            pltpu.VMEM((seq, HD), jnp.bfloat16),
            pltpu.VMEM((seq, HD), jnp.bfloat16),
            pltpu.VMEM((HD, seq), jnp.float32),
            pltpu.VMEM((seq, HD), jnp.bfloat16),
            pltpu.VMEM((seq, HD), jnp.bfloat16),
            pltpu.VMEM((RANK, seq), jnp.float32),
        ],
        compiler_params=pltpu.CompilerParams(dimension_semantics=("arbitrary",)),
        cost_estimate=pl.CostEstimate(
            flops=10 * heads * seq * seq * HD,
            bytes_accessed=16 * seq * heads * HD,
            transcendentals=heads * seq * seq,
        ),
        name="attention_step",
    )(projected, projected, projected, down, down_t, qup, vup, cos, sin, grad_rows)


def local(tokens, norm_gain, w_qkv, a_query, query_up_adapter, a_value, value_up_adapter, out_grad):
    normed = normalize(tokens[0], norm_gain)
    tiles = from_everyone(normed, "tensor")
    gathered = tiles.reshape(-1, normed.shape[1])
    seq = gathered.shape[0]
    weights = lax.all_gather(w_qkv, ("dp", "fsdp"), axis=0, tiled=True)
    projected = jnp.dot(gathered, weights, preferred_element_type=jnp.float32)
    down = jnp.dot(
        gathered, jnp.concatenate([a_query, a_value], 1), preferred_element_type=jnp.float32
    ).astype(jnp.bfloat16)
    grad_rows = lax.all_to_all(out_grad[0], "tensor", split_axis=1, concat_axis=0, tiled=True)
    cos, sin = rotary_tables(seq)
    attended, gbq, gbv, mid_t = attention(
        projected, down, down.T, query_up_adapter, value_up_adapter, cos, sin, grad_rows
    )
    out_rows = lax.all_to_all(attended, "tensor", split_axis=0, concat_axis=1, tiled=True)
    groups = lax.axis_size("tensor")
    own = seq // groups
    mid_split = mid_t.reshape(2 * RANK, groups, own).transpose(1, 0, 2)
    mid = (
        lax.all_to_all(mid_split, "tensor", split_axis=0, concat_axis=0, tiled=True)
        .sum(axis=0)
        .astype(jnp.bfloat16)
    )
    grad_a = ADAPTER_SCALE * dot_nn(mid, normed)
    up = jnp.concatenate([gbq, gbv], 1)
    slots = jnp.zeros((groups, *up.shape), jnp.float32)
    slots = lax.dynamic_update_index_in_dim(slots, up, lax.axis_index("tensor"), 0)
    grad_a, slots = lax.psum((grad_a, slots), ALL)
    up = lax.dynamic_index_in_dim(slots, lax.axis_index("tensor"), 0, keepdims=False)
    return (
        out_rows[None],
        grad_a[:RANK].T,
        up[:, : gbq.shape[1]],
        grad_a[RANK:].T,
        up[:, gbq.shape[1] :],
    )


def solution(mesh):
    return jax.shard_map(
        local,
        mesh=mesh,
        in_specs=(
            P(("dp", "fsdp"), "tensor", None),
            P(),
            P(("dp", "fsdp"), "tensor"),
            P(),
            P(None, "tensor"),
            P(),
            P(None, "tensor"),
            P(("dp", "fsdp"), "tensor", None),
        ),
        out_specs=(
            P(("dp", "fsdp"), "tensor", None),
            P(),
            P(None, "tensor"),
            P(),
            P(None, "tensor"),
        ),
        check_vma=False,
    )
```

time: 587 us -> 411 us (0.70)
  waiting for transfers between devices: 193 us -> 286 us
  matrix products: 115 us -> 32.4 us
  local copies, waits for them, and re-layouts: 98.5 us -> 23.5 us
  blocking collectives: 64 us -> 0 us
  other arithmetic: 63.1 us -> 9.79 us
  Pallas kernels: 0 us -> 26.3 us
  loops' own time: 17.5 us -> 0 us
    psum x1, waiting for transfers between devices: 38.6 us -> 151 us  [local(): grad_a, slots = lax.psum((grad_a, slots), ALL)]
    dot_general x47 -> x1, matrix products: 85.8 us -> 1.69 us  [dot_nn(): return jnp.dot(a, b, preferred_element_type=jnp.float32)]
    psum x1 -> x0, blocking collectives: 64 us -> none  [local(): lax.psum((down_gradient, query_up_gradient, value_up_gradient), ('dp', 'f...]
    dynamic_update_slice x24 -> x1, other arithmetic: 31.9 us -> 0.87 us  [local(): lax.dynamic_update_index_in_dim(slots, up, lax.axis_index('tensor'), 0)]
    dot_general x1 -> x0, local copies, waits for them, and re-layouts: 27 us -> none  [local(): projected = jnp.dot(gathered, weights, preferred_element_type=jnp.float32)]
    pallas_call x0 -> x1, Pallas kernels: none -> 26.3 us  [attention(): pl.pallas_call(functools.partial(attention_kernel, seq), grid=(heads,), i...]
    reduce_sum x17 -> x1, other arithmetic: 23 us -> 0.92 us  [local(): mid = lax.all_to_all(mid_split, 'tensor', split_axis=0, concat_axis=0, ti...]
    another operation x2 -> x0, loops' own time: 17.5 us -> none  [attend(): lax.map(one_head, jnp.arange(kv_heads * QUERY_PER_KV, dtype=jnp.int32))]
  transfers between devices with their start and end apart: 6 -> 6, of which waited for: 4 -> 3; matrix products, arithmetic and copies ran while one was open for 6% -> 13% of each run, Pallas kernels for 0% -> 0%
where the time goes in v1:
time: 411 us; the launch traced here: 410 us
  waiting for transfers between devices  286 us (70%)
  matrix products  32.4 us (8%)
  Pallas kernels  26.3 us (6%)
  local copies, waits for them, and re-layouts  23.5 us (6%)
  starting transfers between devices  18.7 us (5%)
  between operations  14.1 us (3%)
  other arithmetic  9.79 us (2%)
    psum x1, waiting for transfers between devices, local(): grad_a, slots = lax.psum((grad_a, slots), ALL)  151 us
    all_to_all x1, waiting for transfers between devices, from_everyone(): return lax.all_to_all(copies, axis, split_axis=0, concat_axis=0, tiled=True)  129 us
    pallas_call x1, Pallas kernels, attention(): pl.pallas_call(functools.partial(attention_kernel, seq), grid=(heads,), i...  26.3 us
    dot_general x1, matrix products, local(): projected = jnp.dot(gathered, weights, preferred_element_type=jnp.float32)  22.3 us
    dot_general x1, matrix products, local(): jnp.dot(gathered, jnp.concatenate([a_query, a_value], 1), preferred_eleme...  8.4 us
  transfers between devices with their start and end apart: 6, of which 3 were waited for; matrix products, arithmetic and copies ran while one was open for 13% of the time, Pallas kernels for 0%

profile of v1, /device:TPU:1, one launch (start us, length us, event | category | flops | bytes accessed | tf_op | source)
XLA Modules:
  0.0 410.5 jit_solution(13047690376368025441)
XLA Ops:
  7.2 0.0 all-gather.2.cloned.1.call-start
  7.2 0.7 all-gather.2.cloned.1.call-update
  7.9 2.6 fusion
  10.5 2.8 fusion.2
  13.3 6.0 %broadcast_in_dim.17 = bf16[4,192,8192]{2,1,0:T(8,128)(2,1)} broadcast(bf16[192,8192]{1,0:T(8,128)(2,1)S(1)} %fusion.2), dimensions={1,2} | broadcast | bytes 15728640 | tf_op jit(solution)/shard_map/broadcast_in_dim | solution.py:25
  19.3 6.6 %all-to-all-start = ((bf16[4,192,8192]{2,1,0:T(8,128)(2,1)}), bf16[4,192,8192]{2,1,0:T(8,128)(2,1)}, u32[]{:S(2)}, u32[]{:S(2)}) async-start(bf16[4,192,8192]{2,1,0:T(8,128)(2,1)} %broadcast_in_dim.17), calls=%async_computation | async-start | bytes 25165824 | tf_op jit(solution)/shard_map/all_to_all | solution.py:26
  25.9 0.0 copy-start.1
  25.9 3.9 all_to_all.33
  29.8 3.1 copy.16
  32.9 1.5 fusion.8
  34.4 1.2 pad_maximum_fusion
  35.5 129.4 %all-to-all-done = bf16[4,192,8192]{2,1,0:T(8,128)(2,1)} async-done(((bf16[4,192,8192]{2,1,0:T(8,128)(2,1)}), bf16[4,192,8192]{2,1,0:T(8,128)(2,1)}, u32[]{:S(2)}, u32[]{:S(2)}) %all-to-all-start) | async-done | bytes 12582944 | tf_op jit(solution)/shard_map/all_to_all | solution.py:26
  164.9 4.5 %all-to-all-start.1 = ((bf16[192,4,1024]{2,0,1:T(8,128)(2,1)}), bf16[192,4,1024]{2,0,1:T(8,128)(2,1)}, u32[]{:S(2)}, u32[]{:S(2)}) async-start(bf16[192,4,1024]{2,0,1:T(8,128)(2,1)} %copy.16), calls=%async_computation.1 | async-start | bytes 3145728 | tf_op jit(solution)/shard_map/all_to_all | solution.py:214
  169.5 0.0 copy-done.1
  169.5 8.4 %convolution_convert_fusion = bf16[768,32]{0,1:T(8,128)(2,1)S(1)} fusion(bf16[768,8192]{1,0:T(8,128)(2,1)} %bitcast.2, bf16[8192,16]{0,1:T(8,128)(2,1)S(1)} %copy-done.1, bf16[8192,16]{0,1:T(8,128)(2,1)} %param.11), kind=kOutput, calls=%fused_computation.6 | convolution fusion | flops 403726336 | bytes 13156352 | tf_op jit(solution)/shard_map/dot_general | solution.py:211
  177.9 0.0 copy-start.2
  177.9 0.8 copy.17.down_ref
  178.7 0.0 all-gather.2.cloned.1.call-done
  178.7 22.3 %fusion.12.proj_ref.key_ref.value_ref = f32[768,1280]{1,0:T(8,128)} fusion(bf16[768,8192]{1,0:T(8,128)(2,1)} %bitcast.2, bf16[8192,1280]{1,0:T(8,128)(2,1)} %all-gather.2.cloned.1.call-done), kind=kOutput, calls=%fused_computation.26 | convolution fusion | flops 16106127360 | bytes 37486592 | tf_op jit(solution)/shard_map/dot_general | solution.py:210
  201.0 0.0 copy-done.2
  201.1 0.0 all-to-all-done.1
  201.1 26.3 %attention_step.1 = (bf16[768,1024]{1,0:T(8,128)(2,1)}, f32[16,1024]{1,0:T(8,128)}, f32[16,128]{1,0:T(8,128)}, f32[32,768]{1,0:T(8,128)}) custom-call(f32[768,1280]{1,0:T(8,128)} %fusion.12.proj_ref.key_ref.value_ref, f32[768,1280]{1,0:T(8,128)} %fusion.12.proj_ref.key_ref.value_ref, f32[768,1280]{1,0:T(8,128)} %fusion.12.proj_ref.key_ref.value_ref, ...), custom_call_target="tpu_custom_call" | custom-call | flops 6039797760 | bytes 12582912 | tf_op jit(solution)/shard_map/attention_step/pallas_call | solution.py:159
  227.4 1.0 reshape.42
  228.4 0.7 copy.21
  229.1 4.0 all-to-all-start.3
  233.0 0.0 all-reduce.3.cloned.1.call-start
  233.1 0.9 fusion.9
  234.0 0.0 copy-start
  234.0 4.0 all-to-all-done.3
  238.0 0.9 reduce_sum.19
  238.9 1.7 convolution_multiply_fusion
  240.6 0.0 copy-done
  240.6 0.0 all-reduce.3.cloned.1.call-update
  240.6 3.6 all-to-all-start.2
  244.2 151.5 %all-reduce.3.cloned.1.call-done = (f32[32,8192]{1,0:T(8,128)}, f32[4,16,1152]{2,1,0:T(8,128)}) async-done(((f32[32,8192]{1,0:T(8,128)}, f32[4,16,1152]{2,1,0:T(8,128)}), (f32[32,8192]{1,0:T(8,128)}, f32[4,16,1152]{2,1,0:T(8,128)})) %all-reduce.3.cloned.1.call-update) | async-done | bytes 1343504 | tf_op jit(solution)/shard_map/psum | solution.py:232
  395.7 0.9 dynamic-slice_bitcast_fusion
  396.6 0.6 slice.17
  397.2 0.6 slice.19
  397.8 2.2 slice_bitcast_fusion
  400.0 0.0 all-to-all-done.2
  400.0 1.2 copy.18
  401.3 2.4 broadcast_in_dim.18
  (3 shorter events, 0.0 us)
Async XLA Ops:
  7.2 171.6 %all-gather.2.cloned.1.call-start = ((), (), s32[]{:S(2)}) async-start(), calls=%async_computation.4 | async-start | bytes 21626880 | tf_op jit(solution)/shard_map/all_gather | solution.py:209
  19.3 145.6 %all-to-all-start = ((bf16[4,192,8192]{2,1,0:T(8,128)(2,1)}), bf16[4,192,8192]{2,1,0:T(8,128)(2,1)}, u32[]{:S(2)}, u32[]{:S(2)}) async-start(bf16[4,192,8192]{2,1,0:T(8,128)(2,1)} %broadcast_in_dim.17), calls=%async_computation | async-start | bytes 25165824 | tf_op jit(solution)/shard_map/all_to_all | solution.py:26
  25.9 143.6 %copy-start.1 = (bf16[8192,16]{0,1:T(8,128)(2,1)S(1)}, bf16[8192,16]{0,1:T(8,128)(2,1)}, u32[]{:S(2)}) copy-start(bf16[8192,16]{0,1:T(8,128)(2,1)} %param.13) | copy-start | bytes 786436
  164.9 36.1 %all-to-all-start.1 = ((bf16[192,4,1024]{2,0,1:T(8,128)(2,1)}), bf16[192,4,1024]{2,0,1:T(8,128)(2,1)}, u32[]{:S(2)}, u32[]{:S(2)}) async-start(bf16[192,4,1024]{2,0,1:T(8,128)(2,1)} %copy.16), calls=%async_computation.1 | async-start | bytes 3145728 | tf_op jit(solution)/shard_map/all_to_all | solution.py:214
  177.9 23.2 %copy-start.2 = (bf16[768,32]{0,1:T(8,128)(2,1)}, bf16[768,32]{0,1:T(8,128)(2,1)S(1)}, u32[]{:S(2)}) copy-start(bf16[768,32]{0,1:T(8,128)(2,1)S(1)} %convolution_convert_fusion) | copy-start | bytes 147460
  229.1 8.9 %all-to-all-start.3 = ((f32[4,32,192]{2,1,0:T(8,128)}), f32[4,32,192]{2,1,0:T(8,128)}, u32[]{:S(2)}, u32[]{:S(2)}) async-start(f32[4,32,192]{2,1,0:T(8,128)} %bitcast.28), calls=%async_computation.3 | async-start | bytes 262144 | tf_op jit(solution)/shard_map/all_to_all | solution.py:224
  233.0 162.6 %all-reduce.3.cloned.1.call-start = ((), (), s32[]{:S(2)}) async-start(), calls=%async_computation.5 | async-start | bytes 2686976 | tf_op jit(solution)/shard_map/psum | solution.py:232
  234.0 6.6 %copy-start = (f32[4,16,1152]{2,1,0:T(8,128)}, f32[4,16,1152]{2,1,0:T(8,128)S(1)}, u32[]{:S(2)}) copy-start(f32[4,16,1152]{2,1,0:T(8,128)S(1)} %fusion.9) | copy-start | bytes 884740
  240.6 159.4 %all-to-all-start.2 = ((bf16[4,192,1024]{2,1,0:T(8,128)(2,1)}), bf16[4,192,1024]{2,1,0:T(8,128)(2,1)S(1)}, u32[]{:S(2)}, u32[]{:S(2)}) async-start(bf16[4,192,1024]{2,1,0:T(8,128)(2,1)} %bitcast.30), calls=%async_computation.2 | async-start | bytes 3145728 | tf_op jit(solution)/shard_map/all_to_all | solution.py:219
Sparse Core Ops, SparseCore 0:
  9.6 125.2 all-gather.1
  240.7 154.9 all-reduce.2

commit v2 on v1

--- a/solution.py
+++ b/solution.py
@@ -19,17 +19,6 @@
 SCORE_SCALE = 1.0 / math.sqrt(HD)
 LOG2E = 1.4426950408889634
 ALL = ("dp", "fsdp", "tensor")
-
-
-def from_everyone(array, axis):
-    copies = jnp.broadcast_to(array, (lax.axis_size(axis), *array.shape))
-    return lax.all_to_all(copies, axis, split_axis=0, concat_axis=0, tiled=True)
-
-
-def normalize(own_rows, norm_gain):
-    widened = own_rows.astype(jnp.float32)
-    mean_square = jnp.mean(widened * widened, axis=-1, keepdims=True)
-    return (widened * lax.rsqrt(mean_square + EPSILON) * norm_gain).astype(jnp.bfloat16)
 
 
 def rotary_tables(sequence_length):
@@ -201,16 +190,365 @@
     )(projected, projected, projected, down, down_t, qup, vup, cos, sin, grad_rows)
 
 
+MESH = pl.DeviceIdType.MESH
+CHUNKS = 8
+OFFSETS = (0, 3, 1, 2)
+
+
+class Place:
+    def __init__(self):
+        self.dp = lax.axis_index("dp")
+        self.fs = lax.axis_index("fsdp")
+        self.y = lax.axis_index("tensor")
+        self.core = lax.rem(self.dp, 2)
+        self.x = lax.div(self.dp, 2) * 2 + lax.rem(self.fs, 2)
+        self.z = lax.div(self.fs, 2)
+
+    def ring(self, core):
+        first = self.x * (1 - core) + self.z * core
+        second = self.z * (1 - core) + self.x * core
+        return first, second
+
+    def plane(self, core, a, b):
+        first, second = self.ring(core)
+        first = lax.rem(first + a, 4)
+        second = lax.rem(second + b, 4)
+        x = first * (1 - core) + second * core
+        z = second * (1 - core) + first * core
+        return lax.div(x, 2) * 2 + core, z * 2 + lax.rem(x, 2)
+
+    def near(self, a, b):
+        return (*self.plane(self.core, a, b), self.y)
+
+    def along(self, c):
+        return (self.dp, self.fs, lax.rem(self.y + c, 4))
+
+    def partner(self):
+        return (self.dp + 1 - 2 * self.core, self.fs, self.y)
+
+
+def project_kernel(
+    rows,
+    tok_hbm,
+    gain_ref,
+    w_hbm,
+    adapt_ref,
+    proj_hbm,
+    normed_hbm,
+    down_ref,
+    raw,
+    scale_scr,
+    x_buf,
+    w_buf,
+    acc,
+    down_scr,
+    tok_sem,
+    own_sem,
+    out_sem,
+    w_send,
+    w_recv,
+    d_send,
+    d_recv,
+    x_send,
+    x_recv,
+):
+    me = Place()
+    shard = w_hbm.shape[0]
+    half = shard // 2
+    width = tok_hbm.shape[1]
+    wide = width // CHUNKS
+    cols = w_hbm.shape[1]
+    parts = tok_sem.shape[0]
+    part = rows // parts
+
+    def tok_copy(i):
+        piece = pl.ds(i * part, part)
+        return pltpu.make_async_copy(tok_hbm.at[piece], raw.at[piece], tok_sem.at[i])
+
+    for i in range(parts):
+        tok_copy(i).start()
+
+    def block(core, a, b):
+        dp, fs = me.plane(core, a, b)
+        return pl.multiple_of((dp * 8 + fs) * shard, shard)
+
+    own = block(me.core, 0, 0)
+    own_copy = pltpu.make_async_copy(w_hbm, w_buf.at[pl.ds(own, shard)], own_sem)
+    own_copy.start()
+
+    barrier = pltpu.get_barrier_semaphore()
+    neighbours = (
+        me.near(1, 0),
+        me.near(3, 0),
+        me.near(0, 1),
+        me.near(0, 3),
+        me.along(1),
+        me.along(3),
+        me.partner(),
+    )
+    for device in neighbours:
+        pl.semaphore_signal(barrier, inc=1, device_id=device, device_id_type=MESH)
+    pl.semaphore_wait(barrier, len(neighbours))
+
+    sends = []
+
+    def w_copy(a, b, device, kind, way, piece=None, source=None):
+        start = block(me.core, a, b)
+        size = shard
+        if piece is not None:
+            start, size = pl.multiple_of(start + piece * half, half), half
+        dst = w_buf.at[pl.ds(start, size)]
+        return pltpu.make_async_remote_copy(
+            src_ref=dst if source is None else source,
+            dst_ref=dst,
+            send_sem=w_send.at[kind, way],
+            recv_sem=w_recv.at[kind, way],
+            device_id=device,
+            device_id_type=MESH,
+        )
+
+    def w_start(*args, **kwargs):
+        copy = w_copy(*args, **kwargs)
+        copy.start()
+        sends.append(copy)
+
+    def d_copy(core, event, a, b, source=None):
+        dst = w_buf.at[pl.ds(block(core, a, b), shard)]
+        return pltpu.make_async_remote_copy(
+            src_ref=dst if source is None else source,
+            dst_ref=dst,
+            send_sem=d_send.at[event],
+            recv_sem=d_recv.at[event],
+            device_id=me.partner(),
+            device_id_type=MESH,
+        )
+
+    order = []
+
+    def share(a, b, source=None):
+        copy = d_copy(me.core, len(order), a, b, source)
+        copy.start()
+        sends.append(copy)
+        order.append((a, b))
+
+    w_start(0, 0, me.near(1, 0), 4, 0, source=w_hbm)
+    w_start(0, 0, me.near(3, 0), 4, 1, source=w_hbm)
+    w_start(0, 0, me.near(0, 1), 0, 0, source=w_hbm)
+    w_start(0, 0, me.near(0, 3), 0, 1, source=w_hbm)
+    share(0, 0, source=w_hbm)
+
+    for i in range(parts):
+        tok_copy(i).wait()
+
+        @pl.loop(0, part // 16)
+        def _(r):
+            piece = pl.ds(pl.multiple_of(i * part + r * 16, 16), 16)
+            squares = jnp.zeros((16, wide), jnp.float32)
+            for c in range(CHUNKS):
+                value = raw[piece, c * wide : (c + 1) * wide].astype(jnp.float32)
+                squares = squares + value * value
+            mean = jnp.sum(squares, axis=-1, keepdims=True) * (1.0 / width)
+            scale_scr[piece, :] = jnp.broadcast_to(lax.rsqrt(mean + EPSILON), (16, 128))
+
+    def x_copy(row_block, chunk, device, way):
+        ref = x_buf.at[row_block, chunk]
+        return pltpu.make_async_remote_copy(
+            src_ref=ref,
+            dst_ref=ref,
+            send_sem=x_send.at[way, chunk],
+            recv_sem=x_recv.at[way // 2 * 2 if way > 1 else way, chunk],
+            device_id=device,
+            device_id_type=MESH,
+        )
+
+    def normalize_chunk(c):
+        lanes = slice(c * wide, (c + 1) * wide)
+
+        @pl.loop(0, rows // 16)
+        def _(r):
+            piece = pl.ds(pl.multiple_of(r * 16, 16), 16)
+            scale = scale_scr[piece, 0:1]
+            value = raw[piece, lanes].astype(jnp.float32)
+            x_buf[me.y, c, piece, :] = (value * scale * gain_ref[:, lanes]).astype(jnp.bfloat16)
+
+    def x_start(row_block, chunk, device, way):
+        copy = x_copy(row_block, chunk, device, way)
+        copy.start()
+        sends.append(copy)
+
+    middle = CHUNKS // 2
+    for c in range(middle):
+        normalize_chunk(c)
+        normalize_chunk(c + middle)
+        x_start(me.y, c, me.along(1), 0)
+        x_start(me.y, c + middle, me.along(3), 1)
+    for c in range(middle):
+        x_start(me.y, c + middle, me.along(1), 0)
+        x_start(me.y, c, me.along(3), 1)
+
+    acc[...] = jnp.zeros_like(acc)
+    down_scr[...] = jnp.zeros_like(down_scr)
+
+    def normed_copy(c):
+        return pltpu.make_async_copy(x_buf.at[me.y, c], normed_hbm.at[c], out_sem.at[4 + c])
+
+    for c in range(CHUNKS):
+        normed_copy(c).start()
+
+    def arrived(a, b, kind, way, piece=None):
+        w_copy(a, b, me.near(0, 1), kind, way, piece).wait_recv()
+
+    def spread(a, kind):
+        w_start(a, 0, me.near(0, 1), kind, 0)
+        w_start(a, 0, me.near(0, 3), kind, 1)
+
+    own_copy.wait()
+    arrived(3, 0, 4, 0)
+    w_start(3, 0, me.near(1, 0), 4, 2, piece=0)
+    spread(3, 1)
+    share(3, 0)
+    arrived(1, 0, 4, 1)
+    w_start(1, 0, me.near(3, 0), 4, 3, piece=1)
+    spread(1, 2)
+    share(1, 0)
+    for kind, a in enumerate(OFFSETS):
+        if kind == 3:
+            arrived(2, 0, 4, 2, piece=0)
+            arrived(2, 0, 4, 3, piece=1)
+            spread(2, 3)
+            share(2, 0)
+        arrived(a, 3, kind, 0)
+        w_start(a, 3, me.near(0, 1), kind, 2, piece=0)
+        share(a, 3)
+        arrived(a, 1, kind, 1)
+        w_start(a, 1, me.near(0, 3), kind, 3, piece=1)
+        share(a, 1)
+        if kind > 0:
+            before = OFFSETS[kind - 1]
+            arrived(before, 2, kind - 1, 2, piece=0)
+            arrived(before, 2, kind - 1, 3, piece=1)
+            share(before, 2)
+    arrived(OFFSETS[3], 2, 3, 2, piece=0)
+    arrived(OFFSETS[3], 2, 3, 3, piece=1)
+    share(OFFSETS[3], 2)
+
+    minus = lax.rem(me.y + 3, 4)
+    plus = lax.rem(me.y + 1, 4)
+    far = lax.rem(me.y + 2, 4)
+    for c in range(middle):
+        x_copy(minus, c, me.along(1), 0).wait_recv()
+        x_start(minus, c, me.along(1), 2)
+        x_copy(plus, c + middle, me.along(1), 1).wait_recv()
+        x_start(plus, c + middle, me.along(3), 2)
+
+    for event, (a, b) in enumerate(order):
+        d_copy(1 - me.core, event, a, b).wait_recv()
+
+    def multiply(row_block, chunk):
+        value = x_buf[row_block, chunk]
+        lines = pl.ds(pl.multiple_of(row_block * rows, rows), rows)
+        depth = pl.ds(pl.multiple_of(chunk * wide, wide), wide)
+        for n in range(cols // 256):
+            lanes = slice(n * 256, (n + 1) * 256)
+            acc[lines, lanes] += dot_nn(value, w_buf[depth, lanes])
+        down_scr[lines, :] += dot_nt(value, adapt_ref[:, depth])
+
+    def result_copy(i, row_block):
+        lines = pl.ds(pl.multiple_of(row_block * rows, rows), rows)
+        return pltpu.make_async_copy(acc.at[lines], proj_hbm.at[lines], out_sem.at[i])
+
+    @pl.loop(0, CHUNKS)
+    def _(c):
+        multiply(me.y, c)
+
+    result_copy(0, me.y).start()
+
+    @pl.loop(0, CHUNKS)
+    def _(c):
+        @pl.when(c >= middle)
+        def _():
+            x_copy(minus, c, me.along(1), 0).wait_recv()
+
+        multiply(minus, c)
+
+    result_copy(1, minus).start()
+
+    @pl.loop(0, CHUNKS)
+    def _(c):
+        @pl.when(c < middle)
+        def _():
+            x_copy(plus, c, me.along(1), 1).wait_recv()
+
+        multiply(plus, c)
+
+    result_copy(2, plus).start()
+
+    @pl.loop(0, middle)
+    def _(c):
+        x_copy(far, c, me.along(1), 2).wait_recv()
+        multiply(far, c)
+        x_copy(far, c + middle, me.along(1), 2).wait_recv()
+        multiply(far, c + middle)
+
+    result_copy(3, far).start()
+    down_ref[...] = down_scr[...].astype(jnp.bfloat16)
+    for copy in sends:
+        copy.wait_send()
+    for c in range(CHUNKS):
+        normed_copy(c).wait()
+    for i, row_block in enumerate((me.y, minus, plus, far)):
+        result_copy(i, row_block).wait()
+
+
+def gather_project(tokens, gain, w_qkv, adapters_t):
+    rows, width = tokens.shape
+    shard, cols = w_qkv.shape
+    seq = 4 * rows
+    wide = width // CHUNKS
+    anywhere = pl.BlockSpec(memory_space=pl.ANY)
+    inside = pl.BlockSpec(memory_space=pltpu.VMEM)
+    dma = pltpu.SemaphoreType.DMA
+    return pl.pallas_call(
+        functools.partial(project_kernel, rows),
+        in_specs=[anywhere, inside, anywhere, inside],
+        out_specs=[anywhere, anywhere, inside],
+        out_shape=[
+            jax.ShapeDtypeStruct((seq, cols), jnp.float32),
+            jax.ShapeDtypeStruct((CHUNKS, rows, wide), jnp.bfloat16),
+            jax.ShapeDtypeStruct((seq, 2 * RANK), jnp.bfloat16),
+        ],
+        scratch_shapes=[
+            pltpu.VMEM((rows, width), jnp.bfloat16),
+            pltpu.VMEM((rows, 128), jnp.float32),
+            pltpu.VMEM((4, CHUNKS, rows, wide), jnp.bfloat16),
+            pltpu.VMEM((width, cols), jnp.bfloat16),
+            pltpu.VMEM((seq, cols), jnp.float32),
+            pltpu.VMEM((seq, 2 * RANK), jnp.float32),
+            dma((4,)),
+            dma(()),
+            dma((4 + CHUNKS,)),
+            dma((5, 4)),
+            dma((5, 4)),
+            dma((16,)),
+            dma((16,)),
+            dma((3, CHUNKS)),
+            dma((3, CHUNKS)),
+        ],
+        compiler_params=pltpu.CompilerParams(
+            collective_id=1, has_side_effects=True, vmem_limit_bytes=56 << 20
+        ),
+        cost_estimate=pl.CostEstimate(
+            flops=2 * seq * width * cols, bytes_accessed=20 * 1000 * 1000, transcendentals=0
+        ),
+        name="gather_project",
+    )(tokens, gain.reshape(1, width), w_qkv, adapters_t)
+
+
 def local(tokens, norm_gain, w_qkv, a_query, query_up_adapter, a_value, value_up_adapter, out_grad):
-    normed = normalize(tokens[0], norm_gain)
-    tiles = from_everyone(normed, "tensor")
-    gathered = tiles.reshape(-1, normed.shape[1])
-    seq = gathered.shape[0]
-    weights = lax.all_gather(w_qkv, ("dp", "fsdp"), axis=0, tiled=True)
-    projected = jnp.dot(gathered, weights, preferred_element_type=jnp.float32)
-    down = jnp.dot(
-        gathered, jnp.concatenate([a_query, a_value], 1), preferred_element_type=jnp.float32
-    ).astype(jnp.bfloat16)
+    projected, normed, down = gather_project(
+        tokens[0], norm_gain, w_qkv, jnp.concatenate([a_query.T, a_value.T], 0)
+    )
+    seq = projected.shape[0]
     grad_rows = lax.all_to_all(out_grad[0], "tensor", split_axis=1, concat_axis=0, tiled=True)
     cos, sin = rotary_tables(seq)
     attended, gbq, gbv, mid_t = attention(
@@ -225,7 +563,8 @@
         .sum(axis=0)
         .astype(jnp.bfloat16)
     )
-    grad_a = ADAPTER_SCALE * dot_nn(mid, normed)
+    grad_a = ADAPTER_SCALE * jnp.einsum("rp,cpw->rcw", mid, normed, preferred_element_type=jnp.float32)
+    grad_a = grad_a.reshape(2 * RANK, -1)
     up = jnp.concatenate([gbq, gbv], 1)
     slots = jnp.zeros((groups, *up.shape), jnp.float32)
     slots = lax.dynamic_update_index_in_dim(slots, up, lax.axis_index("tensor"), 0)

time: 411 us -> 357 us (0.87)
  waiting for transfers between devices: 286 us -> 154 us
  Pallas kernels: 26.3 us -> 152 us
  matrix products: 32.4 us -> 0.69 us
  starting transfers between devices: 18.7 us -> 12.7 us
  local copies, waits for them, and re-layouts: 23.5 us -> 18 us
  other arithmetic: 9.79 us -> 5.25 us
    all_to_all x1 -> x0, waiting for transfers between devices: 129 us -> none  [from_everyone(): return lax.all_to_all(copies, axis, split_axis=0, concat_axis=0, tiled=True)]
    pallas_call x0 -> x1, Pallas kernels: none -> 125 us  [gather_project(): pl.pallas_call(functools.partial(project_kernel, rows), in_specs=[anywher...]
    dot_general x3 -> x1, matrix products: 32.4 us -> 0.69 us  [local(): jnp.einsum('rp,cpw->rcw', mid, normed, preferred_element_type=jnp.float32)]
    all_to_all x1 -> x0, starting transfers between devices: 6.56 us -> none  [from_everyone(): return lax.all_to_all(copies, axis, split_axis=0, concat_axis=0, tiled=True)]
    broadcast_in_dim x1 -> x0, local copies, waits for them, and re-layouts: 6.01 us -> none  [from_everyone(): copies = jnp.broadcast_to(array, (lax.axis_size(axis), *array.shape))]
  transfers between devices with their start and end apart: 6 -> 4, of which waited for: 3 -> 2; matrix products, arithmetic and copies ran while one was open for 13% -> 3% of each run, Pallas kernels for 0% -> 35%
where the time goes in v2:
time: 357 us
  waiting for transfers between devices  154 us (43%)
  Pallas kernels  152 us (43%)
  local copies, waits for them, and re-layouts  18 us (5%)
  between operations  14.1 us (4%)
  starting transfers between devices  12.7 us (4%)
  other arithmetic  5.25 us (1%)
    psum x1, waiting for transfers between devices, local(): grad_a, slots = lax.psum((grad_a, slots), ALL)  150 us
    pallas_call x1, Pallas kernels, gather_project(): pl.pallas_call(functools.partial(project_kernel, rows), in_specs=[anywher...  125 us
    pallas_call x1, Pallas kernels, attention(): pl.pallas_call(functools.partial(attention_kernel, seq), grid=(heads,), i...  26.4 us
  transfers between devices with their start and end apart: 4, of which 2 were waited for; matrix products, arithmetic and copies ran while one was open for 3% of the time, Pallas kernels for 35%

profile of v2, /device:TPU:1, one launch (start us, length us, event | category | flops | bytes accessed | tf_op | source)
XLA Modules:
  0.0 356.8 jit_solution(1846588193298525719)
XLA Ops:
  7.2 2.9 all_to_all.29
  10.1 1.6 copy.21
  11.7 0.0 copy-start.3
  11.7 0.0 copy-start.4
  11.7 5.1 %all-to-all-start = ((bf16[192,4,1024]{2,0,1:T(8,128)(2,1)}), bf16[192,4,1024]{2,0,1:T(8,128)(2,1)S(1)}, u32[]{:S(2)}, u32[]{:S(2)}) async-start(bf16[192,4,1024]{2,0,1:T(8,128)(2,1)} %copy.21), calls=%async_computation | async-start | bytes 3145728 | tf_op jit(solution)/shard_map/all_to_all | solution.py:552
  16.8 0.0 copy-done.3
  16.8 0.0 copy-done.4
  16.8 0.8 pad_maximum_fusion.adapt_ref
  17.6 125.3 %gather_project.1 = (f32[768,1280]{1,0:T(8,128)}, bf16[8,192,1024]{2,1,0:T(8,128)(2,1)}, bf16[768,32]{1,0:T(8,128)(2,1)}) custom-call(bf16[192,8192]{1,0:T(8,128)(2,1)} %bitcast.36, f32[1,8192]{1,0:T(1,128)} %bitcast.37, bf16[256,1280]{1,0:T(8,128)(2,1)} %w_hbm.1, bf16[32,8192]{1,0:T(8,128)(2,1)} %pad_maximum_fusion.adapt_ref), custom_call_target="tpu_custom_call" | custom-call | flops 16106127360 | bytes 20000000 | tf_op jit(solution)/shard_map/gather_project/pallas_call | solution.py:511
  143.0 1.7 copy.20
  144.6 1.5 fusion.3
  146.1 1.2 pad_maximum_fusion.1
  147.3 0.0 all-to-all-done
  147.3 0.0 copy-start.1
  147.3 1.1 copy-done.1
  148.4 0.0 copy-start
  148.4 26.4 %attention_step.1 = (bf16[768,1024]{1,0:T(8,128)(2,1)}, f32[16,1024]{1,0:T(8,128)}, f32[16,128]{1,0:T(8,128)}, f32[32,768]{1,0:T(8,128)}) custom-call(f32[768,1280]{1,0:T(8,128)} %get-tuple-element.12.proj_ref.key_ref.value_ref, f32[768,1280]{1,0:T(8,128)} %get-tuple-element.12.proj_ref.key_ref.value_ref, ...), custom_call_target="tpu_custom_call" | custom-call | flops 6039797760 | bytes 12582912 | tf_op jit(solution)/shard_map/attention_step/pallas_call | solution.py:148
  174.8 1.0 reshape.34
  175.9 0.7 copy.27
  176.5 3.9 %all-to-all-start.2 = ((f32[4,32,192]{2,1,0:T(8,128)}), f32[4,32,192]{2,1,0:T(8,128)}, u32[]{:S(2)}, u32[]{:S(2)}) async-start(f32[4,32,192]{2,1,0:T(8,128)} %bitcast.29), calls=%async_computation.2 | async-start | bytes 262144 | tf_op jit(solution)/shard_map/all_to_all | solution.py:562
  180.5 0.0 all-reduce.3.cloned.1.call-start
  180.6 0.9 fusion.4
  181.4 0.0 copy-start.2
  181.4 3.9 %all-to-all-done.2 = f32[4,32,192]{2,1,0:T(8,128)} async-done(((f32[4,32,192]{2,1,0:T(8,128)}), f32[4,32,192]{2,1,0:T(8,128)}, u32[]{:S(2)}, u32[]{:S(2)}) %all-to-all-start.2) | async-done | bytes 98336 | tf_op jit(solution)/shard_map/all_to_all | solution.py:562
  185.4 0.9 reduce_sum.9
  186.3 0.0 copy-done
  186.3 0.7 fusion
  187.0 0.0 copy-done.2
  187.0 1.0 copy.25
  188.1 0.0 all-reduce.3.cloned.1.call-update
  188.1 3.6 %all-to-all-start.1 = ((bf16[4,192,1024]{2,1,0:T(8,128)(2,1)}), bf16[4,192,1024]{2,1,0:T(8,128)(2,1)S(1)}, u32[]{:S(2)}, u32[]{:S(2)}) async-start(bf16[4,192,1024]{2,1,0:T(8,128)(2,1)} %bitcast.7), calls=%async_computation.1 | async-start | bytes 3145728 | tf_op jit(solution)/shard_map/all_to_all | solution.py:557
  191.7 150.4 %all-reduce.3.cloned.1.call-done = (f32[32,8192]{1,0:T(8,128)}, f32[4,16,1152]{2,1,0:T(8,128)}) async-done(((f32[32,8192]{1,0:T(8,128)}, f32[4,16,1152]{2,1,0:T(8,128)}), (f32[32,8192]{1,0:T(8,128)}, f32[4,16,1152]{2,1,0:T(8,128)})) %all-reduce.3.cloned.1.call-update) | async-done | bytes 1343504 | tf_op jit(solution)/shard_map/psum | solution.py:571
  342.0 0.9 dynamic-slice_bitcast_fusion
  342.9 0.6 slice.17
  343.6 0.6 slice.19
  344.2 2.2 slice_bitcast_fusion
  346.4 0.0 all-to-all-done.1
  346.4 1.2 copy.22
  347.6 2.4 broadcast_in_dim.12
  (2 shorter events, 0.0 us)
Async XLA Ops:
  11.7 5.1 %copy-start.3 = (bf16[8192,16]{0,1:T(8,128)(2,1)S(1)}, bf16[8192,16]{0,1:T(8,128)(2,1)}, u32[]{:S(2)}) copy-start(bf16[8192,16]{0,1:T(8,128)(2,1)} %param.13) | copy-start | bytes 786436
  11.7 5.1 %copy-start.4 = (bf16[8192,16]{0,1:T(8,128)(2,1)S(1)}, bf16[8192,16]{0,1:T(8,128)(2,1)}, u32[]{:S(2)}) copy-start(bf16[8192,16]{0,1:T(8,128)(2,1)} %param.11) | copy-start | bytes 786436
  11.7 135.6 %all-to-all-start = ((bf16[192,4,1024]{2,0,1:T(8,128)(2,1)}), bf16[192,4,1024]{2,0,1:T(8,128)(2,1)S(1)}, u32[]{:S(2)}, u32[]{:S(2)}) async-start(bf16[192,4,1024]{2,0,1:T(8,128)(2,1)} %copy.21), calls=%async_computation | async-start | bytes 3145728 | tf_op jit(solution)/shard_map/all_to_all | solution.py:552
  147.3 1.1 copy-start.1
  148.4 37.9 %copy-start = (bf16[8,192,1024]{2,1,0:T(8,128)(2,1)S(1)}, bf16[8,192,1024]{2,1,0:T(8,128)(2,1)}, u32[]{:S(2)}) copy-start(bf16[8,192,1024]{2,1,0:T(8,128)(2,1)} %get-tuple-element.16) | copy-start | bytes 9437188
  176.5 8.8 %all-to-all-start.2 = ((f32[4,32,192]{2,1,0:T(8,128)}), f32[4,32,192]{2,1,0:T(8,128)}, u32[]{:S(2)}, u32[]{:S(2)}) async-start(f32[4,32,192]{2,1,0:T(8,128)} %bitcast.29), calls=%async_computation.2 | async-start | bytes 262144 | tf_op jit(solution)/shard_map/all_to_all | solution.py:562
  180.5 161.5 %all-reduce.3.cloned.1.call-start = ((), (), s32[]{:S(2)}) async-start(), calls=%async_computation.3 | async-start | bytes 2686976 | tf_op jit(solution)/shard_map/psum | solution.py:571
  181.4 5.6 %copy-start.2 = (f32[4,16,1152]{2,1,0:T(8,128)}, f32[4,16,1152]{2,1,0:T(8,128)S(1)}, u32[]{:S(2)}) copy-start(f32[4,16,1152]{2,1,0:T(8,128)S(1)} %fusion.4) | copy-start | bytes 884740
  188.1 158.3 %all-to-all-start.1 = ((bf16[4,192,1024]{2,1,0:T(8,128)(2,1)}), bf16[4,192,1024]{2,1,0:T(8,128)(2,1)S(1)}, u32[]{:S(2)}, u32[]{:S(2)}) async-start(bf16[4,192,1024]{2,1,0:T(8,128)(2,1)} %bitcast.7), calls=%async_computation.1 | async-start | bytes 3145728 | tf_op jit(solution)/shard_map/all_to_all | solution.py:557
Sparse Core Ops, SparseCore 0:
  188.2 153.7 all-reduce.2

commit v3 on v2

--- a/solution.py
+++ b/solution.py
@@ -3,6 +3,7 @@
 
 import jax
 import jax.numpy as jnp
+import numpy as np
 from jax import lax
 from jax.experimental import pallas as pl
 from jax.experimental.pallas import tpu as pltpu
@@ -18,17 +19,17 @@
 ROPE_BASE = 500000.0
 SCORE_SCALE = 1.0 / math.sqrt(HD)
 LOG2E = 1.4426950408889634
-ALL = ("dp", "fsdp", "tensor")
 
 
 def rotary_tables(sequence_length):
     half_dim = HD // 2
-    positions = jnp.arange(sequence_length, dtype=jnp.float32)[:, None]
-    inv_freq = ROPE_BASE ** (-jnp.arange(half_dim, dtype=jnp.float32) / half_dim)
-    angles = positions * inv_freq
-    cosine = jnp.cos(angles)
-    sine = jnp.sin(angles)
-    return jnp.concatenate([cosine, cosine], 1), jnp.concatenate([-sine, sine], 1)
+    inv_freq = ROPE_BASE ** (-np.arange(half_dim) / half_dim)
+    angles = np.arange(sequence_length)[:, None] * inv_freq
+    cosine, sine = np.cos(angles), np.sin(angles)
+    return (
+        np.concatenate([cosine, cosine], 1).astype(np.float32),
+        np.concatenate([-sine, sine], 1).astype(np.float32),
+    )
 
 
 def dot_nt(a, b):
@@ -41,153 +42,6 @@
 
 def rotate(x, cos, sin):
     return x * cos + pltpu.roll(x, HD // 2, 1) * sin
-
-
-def attention_kernel(
-    seq,
-    proj_ref,
-    key_ref,
-    value_ref,
-    down_ref,
-    down_t_ref,
-    qup_ref,
-    vup_ref,
-    cos_ref,
-    sin_ref,
-    grad_ref,
-    out_ref,
-    gbq_ref,
-    gbv_ref,
-    mid_t_ref,
-    k_scr,
-    v_scr,
-    dv_scr,
-    q_scr,
-    dq_scr,
-    mid_scr,
-):
-    head = pl.program_id(0)
-    blocks = seq // QB
-
-    @pl.when(head == 0)
-    def _():
-        k_scr[...] = rotate(
-            key_ref[...].astype(jnp.bfloat16).astype(jnp.float32), cos_ref[...], sin_ref[...]
-        ).astype(jnp.bfloat16)
-        v_scr[...] = (
-            value_ref[...] + ADAPTER_SCALE * dot_nn(down_ref[:, RANK:], vup_ref[...])
-        ).astype(jnp.bfloat16)
-        dv_scr[...] = jnp.zeros_like(dv_scr)
-        mid_scr[...] = jnp.zeros_like(mid_scr)
-
-    queries = (proj_ref[...] + ADAPTER_SCALE * dot_nn(down_ref[:, :RANK], qup_ref[...])).astype(
-        jnp.bfloat16
-    )
-    q_scr[...] = rotate(queries.astype(jnp.float32), cos_ref[...], sin_ref[...]).astype(
-        jnp.bfloat16
-    )
-    row = lax.broadcasted_iota(jnp.int32, (QB, QB), 0)
-    col = lax.broadcasted_iota(jnp.int32, (QB, QB), 1)
-    causal = row >= col
-    factor = SCORE_SCALE * LOG2E
-    for i in range(blocks):
-        rows = slice(i * QB, (i + 1) * QB)
-        q = q_scr[rows, :]
-        grad = grad_ref[rows, :]
-        grad_t = grad.T
-        scores = []
-        for j in range(i + 1):
-            s = dot_nt(q, k_scr[j * QB : (j + 1) * QB, :])
-            if j == i:
-                s = jnp.where(causal, s, -1e30)
-            scores.append(s)
-        top = functools.reduce(jnp.maximum, scores)
-        top = jnp.max(top, axis=-1, keepdims=True) * factor
-        weights = [jnp.exp2(s * factor - top) for s in scores]
-        total = jnp.sum(functools.reduce(jnp.add, weights), axis=-1, keepdims=True)
-        inverse = 1.0 / total
-        probs = [w * inverse for w in weights]
-        rounded = [p.astype(jnp.bfloat16) for p in probs]
-        attended = functools.reduce(
-            jnp.add, [dot_nn(rounded[j], v_scr[j * QB : (j + 1) * QB, :]) for j in range(i + 1)]
-        )
-        out_ref[rows, :] = attended.astype(jnp.bfloat16)
-        prods = []
-        for j in range(i + 1):
-            keys = slice(j * QB, (j + 1) * QB)
-            dp = dot_nt(grad, v_scr[keys, :])
-            prods.append(probs[j] * dp)
-            dv_scr[:, keys] += dot_nn(grad_t, rounded[j])
-        inner = jnp.sum(functools.reduce(jnp.add, prods), axis=-1, keepdims=True)
-        ds = [(prods[j] - probs[j] * inner).astype(jnp.bfloat16) for j in range(i + 1)]
-        dq = functools.reduce(
-            jnp.add, [dot_nn(ds[j], k_scr[j * QB : (j + 1) * QB, :]) for j in range(i + 1)]
-        )
-        dq = (dq * SCORE_SCALE).astype(jnp.bfloat16).astype(jnp.float32)
-        dq_scr[rows, :] = rotate(dq, cos_ref[rows, :], -sin_ref[rows, :]).astype(jnp.bfloat16)
-    dq = dq_scr[...]
-    gbq_ref[...] = ADAPTER_SCALE * dot_nn(down_t_ref[:RANK, :], dq)
-    mid_scr[...] += dot_nt(qup_ref[...], dq)
-
-    @pl.when(head == QUERY_PER_KV - 1)
-    def _():
-        dv = dv_scr[...].T.astype(jnp.bfloat16)
-        gbv_ref[...] = ADAPTER_SCALE * dot_nn(down_t_ref[RANK:, :], dv)
-        mid_t_ref[:RANK, :] = mid_scr[...]
-        mid_t_ref[RANK:, :] = dot_nt(vup_ref[...], dv)
-
-
-def attention(projected, down, down_t, qup, vup, cos, sin, grad_rows):
-    seq = projected.shape[0]
-    heads = QUERY_PER_KV
-
-    def whole(shape):
-        return pl.BlockSpec(shape, lambda h: (0, 0))
-
-    column = lambda h: (0, h)
-    return pl.pallas_call(
-        functools.partial(attention_kernel, seq),
-        grid=(heads,),
-        in_specs=[
-            pl.BlockSpec((seq, HD), column),
-            pl.BlockSpec((seq, HD), lambda h: (0, heads)),
-            pl.BlockSpec((seq, HD), lambda h: (0, heads + 1)),
-            whole((seq, 2 * RANK)),
-            whole((2 * RANK, seq)),
-            pl.BlockSpec((RANK, HD), column),
-            whole((RANK, HD)),
-            whole((seq, HD)),
-            whole((seq, HD)),
-            pl.BlockSpec((seq, HD), column),
-        ],
-        out_specs=[
-            pl.BlockSpec((seq, HD), column),
-            pl.BlockSpec((RANK, HD), column),
-            whole((RANK, HD)),
-            whole((2 * RANK, seq)),
-        ],
-        out_shape=[
-            jax.ShapeDtypeStruct((seq, heads * HD), jnp.bfloat16),
-            jax.ShapeDtypeStruct((RANK, heads * HD), jnp.float32),
-            jax.ShapeDtypeStruct((RANK, HD), jnp.float32),
-            jax.ShapeDtypeStruct((2 * RANK, seq), jnp.float32),
-        ],
-        scratch_shapes=[
-            pltpu.VMEM((seq, HD), jnp.bfloat16),
-            pltpu.VMEM((seq, HD), jnp.bfloat16),
-            pltpu.VMEM((HD, seq), jnp.float32),
-            pltpu.VMEM((seq, HD), jnp.bfloat16),
-            pltpu.VMEM((seq, HD), jnp.bfloat16),
-            pltpu.VMEM((RANK, seq), jnp.float32),
-        ],
-        compiler_params=pltpu.CompilerParams(dimension_semantics=("arbitrary",)),
-        cost_estimate=pl.CostEstimate(
-            flops=10 * heads * seq * seq * HD,
-            bytes_accessed=16 * seq * heads * HD,
-            transcendentals=heads * seq * seq,
-        ),
-        name="attention_step",
-    )(projected, projected, projected, down, down_t, qup, vup, cos, sin, grad_rows)
 
 
 MESH = pl.DeviceIdType.MESH
@@ -544,39 +398,492 @@
     )(tokens, gain.reshape(1, width), w_qkv, adapters_t)
 
 
+CHIPS = 64
+PLANE = 16
+
+
+def attention_kernel(
+    seq,
+    proj_ref,
+    key_ref,
+    value_ref,
+    down_ref,
+    qup_ref,
+    vup_ref,
+    cos_ref,
+    sin_ref,
+    grad_hbm,
+    normed_hbm,
+    out_hbm,
+    ga_q_hbm,
+    ga_v_hbm,
+    gb_q_hbm,
+    gb_v_hbm,
+    k_scr,
+    v_scr,
+    dv_scr,
+    q_scr,
+    dq_scr,
+    down_t,
+    mid_scr,
+    mid_recv,
+    stage,
+    g_buf,
+    o_buf,
+    n_buf,
+    part,
+    part_recv,
+    total,
+    rs_recv,
+    final,
+    res,
+    up_part,
+    up_recv,
+    up_total,
+    up_rs,
+    up_final,
+    up_res,
+    local_sem,
+    own_sem,
+    o_own_sem,
+    g_send,
+    g_recv,
+    o_send,
+    o_recv,
+    m_send,
+    m_recv,
+    c_send,
+    c_recv,
+    r_send,
+    r_recv,
+):
+    me = Place()
+    head = pl.program_id(0)
+    heads = QUERY_PER_KV
+    rows = seq // 4
+    group = heads * HD
+    blocks = seq // QB
+    plane = lax.div(me.dp, 2) * 8 + me.fs
+    chip = plane * 4 + me.y
+
+    def lines(block):
+        return pl.ds(pl.multiple_of(block * rows, rows), rows)
+
+    def columns(block, h):
+        return pl.ds(pl.multiple_of(block * group + h * HD, HD), HD)
+
+    def remote(src, dst, send, recv, device):
+        return pltpu.make_async_remote_copy(
+            src_ref=src,
+            dst_ref=dst,
+            send_sem=send,
+            recv_sem=recv,
+            device_id=device,
+            device_id_type=MESH,
+        )
+
+    def of_chip(index):
+        at = lax.div(index, 4)
+        return (lax.div(at, 8) * 2 + me.core, lax.rem(at, 8), lax.rem(index, 4))
+
+    stage_copy = pltpu.make_async_copy(grad_hbm, stage, local_sem.at[0])
+    normed_copy = pltpu.make_async_copy(normed_hbm, n_buf, local_sem.at[1])
+
+    def own_grad(h):
+        return pltpu.make_async_copy(
+            grad_hbm.at[:, columns(me.y, h)], g_buf.at[h, lines(me.y)], own_sem.at[h]
+        )
+
+    def grad_copy(h, c):
+        to = lax.rem(me.y + c, 4)
+        return remote(
+            stage.at[:, columns(to, h)],
+            g_buf.at[h, lines(me.y)],
+            g_send.at[h, c - 1],
+            g_recv.at[h, c - 1],
+            me.along(c),
+        )
+
+    def grad_arrival(h, c):
+        ref = g_buf.at[h, lines(lax.rem(me.y + 4 - c, 4))]
+        return remote(ref, ref, g_send.at[h, c - 1], g_recv.at[h, c - 1], me.along(c))
+
+    def own_out(h):
+        return pltpu.make_async_copy(
+            o_buf.at[h, lines(me.y)], out_hbm.at[:, columns(me.y, h)], o_own_sem.at[h]
+        )
+
+    def out_copy(h, c):
+        to = lax.rem(me.y + c, 4)
+        return remote(
+            o_buf.at[h, lines(to)],
+            out_hbm.at[:, columns(me.y, h)],
+            o_send.at[h, c - 1],
+            o_recv.at[h, c - 1],
+            me.along(c),
+        )
+
+    def out_arrival(h, c):
+        ref = out_hbm.at[:, columns(lax.rem(me.y + 4 - c, 4), h)]
+        return remote(ref, ref, o_send.at[h, c - 1], o_recv.at[h, c - 1], me.along(c))
+
+    @pl.when(head == 0)
+    def _():
+        stage_copy.start()
+        barrier = pltpu.get_barrier_semaphore()
+
+        @pl.loop(1, CHIPS)
+        def _(o):
+            pl.semaphore_signal(
+                barrier, inc=1, device_id=of_chip(lax.rem(chip + o, CHIPS)), device_id_type=MESH
+            )
+
+        pl.semaphore_signal(barrier, inc=1, device_id=me.partner(), device_id_type=MESH)
+
+        @pl.loop(0, heads)
+        def _(h):
+            own_grad(h).start()
+
+        normed_copy.start()
+        stage_copy.wait()
+        pl.semaphore_wait(barrier, CHIPS)
+
+        @pl.loop(0, heads)
+        def _(h):
+            for c in (1, 3, 2):
+                grad_copy(h, c).start()
+
+        k_scr[...] = rotate(
+            key_ref[...].astype(jnp.bfloat16).astype(jnp.float32), cos_ref[...], sin_ref[...]
+        ).astype(jnp.bfloat16)
+        v_scr[...] = (
+            value_ref[...] + ADAPTER_SCALE * dot_nn(down_ref[:, RANK:], vup_ref[...])
+        ).astype(jnp.bfloat16)
+        down_t[...] = down_ref[...].astype(jnp.float32).T.astype(jnp.bfloat16)
+        dv_scr[...] = jnp.zeros_like(dv_scr)
+        mid_scr[...] = jnp.zeros_like(mid_scr)
+        up_part[...] = jnp.zeros_like(up_part)
+
+    queries = (proj_ref[...] + ADAPTER_SCALE * dot_nn(down_ref[:, :RANK], qup_ref[...])).astype(
+        jnp.bfloat16
+    )
+    q_scr[...] = rotate(queries.astype(jnp.float32), cos_ref[...], sin_ref[...]).astype(
+        jnp.bfloat16
+    )
+    own_grad(head).wait()
+    for c in (1, 3, 2):
+        grad_arrival(head, c).wait_recv()
+
+    row = lax.broadcasted_iota(jnp.int32, (QB, QB), 0)
+    col = lax.broadcasted_iota(jnp.int32, (QB, QB), 1)
+    causal = row >= col
+    factor = SCORE_SCALE * LOG2E
+    for i in range(blocks):
+        own_rows = slice(i * QB, (i + 1) * QB)
+        q = q_scr[own_rows, :]
+        grad = g_buf[head, own_rows, :]
+        grad_t = grad.T
+        scores = []
+        for j in range(i + 1):
+            s = dot_nt(q, k_scr[j * QB : (j + 1) * QB, :])
+            if j == i:
+                s = jnp.where(causal, s, -1e30)
+            scores.append(s)
+        top = functools.reduce(jnp.maximum, scores)
+        top = jnp.max(top, axis=-1, keepdims=True) * factor
+        weights = [jnp.exp2(s * factor - top) for s in scores]
+        whole = jnp.sum(functools.reduce(jnp.add, weights), axis=-1, keepdims=True)
+        inverse = 1.0 / whole
+        probs = [w * inverse for w in weights]
+        rounded = [p.astype(jnp.bfloat16) for p in probs]
+        attended = functools.reduce(
+            jnp.add, [dot_nn(rounded[j], v_scr[j * QB : (j + 1) * QB, :]) for j in range(i + 1)]
+        )
+        o_buf[head, own_rows, :] = attended.astype(jnp.bfloat16)
+        prods = []
+        for j in range(i + 1):
+            keys = slice(j * QB, (j + 1) * QB)
+            dp = dot_nt(grad, v_scr[keys, :])
+            prods.append(probs[j] * dp)
+            dv_scr[:, keys] += dot_nn(grad_t, rounded[j])
+        inner = jnp.sum(functools.reduce(jnp.add, prods), axis=-1, keepdims=True)
+        ds = [(prods[j] - probs[j] * inner).astype(jnp.bfloat16) for j in range(i + 1)]
+        dq = functools.reduce(
+            jnp.add, [dot_nn(ds[j], k_scr[j * QB : (j + 1) * QB, :]) for j in range(i + 1)]
+        )
+        dq = (dq * SCORE_SCALE).astype(jnp.bfloat16).astype(jnp.float32)
+        dq_scr[own_rows, :] = rotate(dq, cos_ref[own_rows, :], -sin_ref[own_rows, :]).astype(
+            jnp.bfloat16
+        )
+
+    own_out(head).start()
+    for c in (1, 3, 2):
+        out_copy(head, c).start()
+    up = dot_nn(down_t[:RANK, :], dq_scr[...])
+    up_part[0, head] = up[:8]
+    up_part[1, head] = up[8:]
+    for b in range(4):
+        mid_scr[b, :RANK, :] += dot_nt(qup_ref[...], dq_scr[b * rows : (b + 1) * rows, :])
+
+    @pl.when(head == heads - 1)
+    def _():
+        dv = dv_scr[...].T.astype(jnp.bfloat16)
+        for b in range(4):
+            mid_scr[b, RANK:, :] = dot_nt(vup_ref[...], dv[b * rows : (b + 1) * rows])
+        up = dot_nn(down_t[RANK:, :], dv)
+        up_part[0, heads] = up[:8]
+        up_part[1, heads] = up[8:]
+
+        def mid_copy(c):
+            return remote(
+                mid_scr.at[lax.rem(me.y + c, 4)],
+                mid_recv.at[c - 1],
+                m_send.at[c - 1],
+                m_recv.at[c - 1],
+                me.along(c),
+            )
+
+        for c in (1, 3, 2):
+            mid_copy(c).start()
+        up_swap = remote(
+            up_part.at[1 - me.core], up_recv, c_send.at[0], c_recv.at[0], me.partner()
+        )
+        up_swap.start()
+        normed_copy.wait()
+        for c in (1, 3, 2):
+            mid_copy(c).wait_recv()
+        mid = (mid_scr[me.y] + mid_recv[0] + mid_recv[1] + mid_recv[2]).astype(jnp.bfloat16)
+
+        def partial(half):
+            @pl.loop(0, 4)
+            def _(n):
+                made = dot_nn(mid, n_buf[half * 4 + n])
+                for r in range(4):
+                    for k in range(4):
+                        part[half * CHIPS + r * 16 + n * 4 + k] = made[
+                            r * 8 : (r + 1) * 8, k * 256 : (k + 1) * 256
+                        ]
+
+        def of_half(half):
+            return pl.ds(pl.multiple_of(half * CHIPS, CHIPS), CHIPS)
+
+        partial(1 - me.core)
+        swap = remote(
+            part.at[of_half(1 - me.core)], part_recv, c_send.at[1], c_recv.at[1], me.partner()
+        )
+        swap.start()
+        partial(me.core)
+        up_swap.wait_recv()
+        up_total[...] = up_part[me.core] + up_recv[...]
+        swap.wait_recv()
+
+        @pl.loop(0, CHIPS // 8)
+        def _(n):
+            piece = pl.ds(pl.multiple_of(n * 8, 8), 8)
+            mine = pl.ds(pl.multiple_of(me.core * CHIPS + n * 8, 8), 8)
+            total[piece] = part[mine] + part_recv[piece]
+
+        @pl.loop(1, PLANE)
+        def _(o):
+            to = lax.rem(plane + o, PLANE)
+            remote(
+                up_total.at[to], up_rs.at[o - 1], r_send.at[1], r_recv.at[1], of_chip(to * 4 + me.y)
+            ).start()
+
+        @pl.loop(1, CHIPS)
+        def _(o):
+            to = lax.rem(chip + o, CHIPS)
+            remote(
+                total.at[to], rs_recv.at[o - 1], r_send.at[0], r_recv.at[0], of_chip(to)
+            ).start()
+
+        up_many = remote(up_rs, up_rs, r_send.at[1], r_recv.at[1], me.partner())
+        many = remote(rs_recv, rs_recv, r_send.at[0], r_recv.at[0], me.partner())
+        up_many.wait_recv()
+        up_sum = lax.fori_loop(
+            0, PLANE - 1, lambda o, value: value + up_rs[o], up_total[plane], unroll=True
+        )
+        up_final[...] = ADAPTER_SCALE * up_sum
+        many.wait_recv()
+        summed = lax.fori_loop(0, CHIPS - 1, lambda o, value: value + rs_recv[o], total[chip])
+        final[...] = ADAPTER_SCALE * summed
+
+        def place(at):
+            r = pl.multiple_of(lax.div(at, 16) * 8, 8)
+            k = pl.multiple_of(me.core * 4096 + lax.rem(at, 16) * 256, 256)
+            return res.at[pl.ds(r, 8), pl.ds(k, 256)]
+
+        def up_place(at):
+            return up_res.at[me.core, :, pl.ds(pl.multiple_of(at * HD, HD), HD)]
+
+        @pl.loop(1, PLANE)
+        def _(o):
+            to = lax.rem(plane + o, PLANE)
+            remote(
+                up_final, up_place(plane), r_send.at[3], r_recv.at[3], of_chip(to * 4 + me.y)
+            ).start()
+
+        @pl.loop(1, CHIPS)
+        def _(o):
+            to = lax.rem(chip + o, CHIPS)
+            remote(final, place(chip), r_send.at[2], r_recv.at[2], of_chip(to)).start()
+
+        r = pl.multiple_of(lax.div(chip, 16) * 8, 8)
+        k = pl.multiple_of(me.core * 4096 + lax.rem(chip, 16) * 256, 256)
+        res[pl.ds(r, 8), pl.ds(k, 256)] = final[...]
+        up_res[me.core, :, pl.ds(pl.multiple_of(plane * HD, HD), HD)] = up_final[...]
+        up_all = remote(up_rs, up_rs, r_send.at[3], r_recv.at[3], me.partner())
+        all_of = remote(rs_recv, rs_recv, r_send.at[2], r_recv.at[2], me.partner())
+        up_all.wait_recv()
+        up_half = remote(
+            up_res.at[me.core], up_res.at[me.core], c_send.at[2], c_recv.at[2], me.partner()
+        )
+        up_half.start()
+        all_of.wait_recv()
+        kept = res.at[:, pl.ds(pl.multiple_of(me.core * 4096, 4096), 4096)]
+        other = res.at[:, pl.ds(pl.multiple_of((1 - me.core) * 4096, 4096), 4096)]
+        half = remote(kept, kept, c_send.at[3], c_recv.at[3], me.partner())
+        half.start()
+        up_other = up_res.at[1 - me.core]
+        remote(up_other, up_other, c_send.at[2], c_recv.at[2], me.partner()).wait_recv()
+        remote(other, other, c_send.at[3], c_recv.at[3], me.partner()).wait_recv()
+        writes = [
+            pltpu.make_async_copy(res.at[pl.ds(0, RANK)], ga_q_hbm, local_sem.at[2]),
+            pltpu.make_async_copy(res.at[pl.ds(RANK, RANK)], ga_v_hbm, local_sem.at[3]),
+        ]
+        for b in range(2):
+            writes.append(
+                pltpu.make_async_copy(
+                    up_res.at[b, :, pl.ds(0, group)],
+                    gb_q_hbm.at[pl.ds(8 * b, 8)],
+                    local_sem.at[4 + b],
+                )
+            )
+            writes.append(
+                pltpu.make_async_copy(
+                    up_res.at[b, :, pl.ds(group, HD)],
+                    gb_v_hbm.at[pl.ds(8 * b, 8)],
+                    local_sem.at[6 + b],
+                )
+            )
+        for copy in writes:
+            copy.start()
+
+        @pl.loop(0, heads)
+        def _(h):
+            own_out(h).wait()
+            for c in (1, 3, 2):
+                grad_copy(h, c).wait_send()
+                out_copy(h, c).wait_send()
+                out_arrival(h, c).wait_recv()
+
+        for c in (1, 3, 2):
+            mid_copy(c).wait_send()
+        for copy in (up_swap, swap, many, up_many, all_of, up_all, up_half, half):
+            copy.wait_send()
+        for copy in writes:
+            copy.wait()
+
+
+def attention(projected, down, qup, vup, cos, sin, out_grad, normed):
+    seq = projected.shape[0]
+    heads = QUERY_PER_KV
+    rows = seq // 4
+    width = normed.shape[0] * normed.shape[2]
+
+    def whole(shape):
+        return pl.BlockSpec(shape, lambda h: (0, 0))
+
+    anywhere = pl.BlockSpec(memory_space=pl.ANY)
+    column = lambda h: (0, h)
+    dma = pltpu.SemaphoreType.DMA
+    f32, bf16 = jnp.float32, jnp.bfloat16
+    return pl.pallas_call(
+        functools.partial(attention_kernel, seq),
+        grid=(heads,),
+        in_specs=[
+            pl.BlockSpec((seq, HD), column),
+            pl.BlockSpec((seq, HD), lambda h: (0, heads)),
+            pl.BlockSpec((seq, HD), lambda h: (0, heads + 1)),
+            whole((seq, 2 * RANK)),
+            pl.BlockSpec((RANK, HD), column),
+            whole((RANK, HD)),
+            whole((seq, HD)),
+            whole((seq, HD)),
+            anywhere,
+            anywhere,
+        ],
+        out_specs=[anywhere] * 5,
+        out_shape=[
+            jax.ShapeDtypeStruct((rows, 4 * heads * HD), bf16),
+            jax.ShapeDtypeStruct((RANK, width), f32),
+            jax.ShapeDtypeStruct((RANK, width), f32),
+            jax.ShapeDtypeStruct((RANK, heads * HD), f32),
+            jax.ShapeDtypeStruct((RANK, HD), f32),
+        ],
+        scratch_shapes=[
+            pltpu.VMEM((seq, HD), bf16),
+            pltpu.VMEM((seq, HD), bf16),
+            pltpu.VMEM((HD, seq), f32),
+            pltpu.VMEM((seq, HD), bf16),
+            pltpu.VMEM((seq, HD), bf16),
+            pltpu.VMEM((2 * RANK, seq), bf16),
+            pltpu.VMEM((4, 2 * RANK, rows), f32),
+            pltpu.VMEM((3, 2 * RANK, rows), f32),
+            pltpu.VMEM((rows, 4 * heads * HD), bf16),
+            pltpu.VMEM((heads, seq, HD), bf16),
+            pltpu.VMEM((heads, seq, HD), bf16),
+            pltpu.VMEM(normed.shape, bf16),
+            pltpu.VMEM((2 * CHIPS, 8, 256), f32),
+            pltpu.VMEM((CHIPS, 8, 256), f32),
+            pltpu.VMEM((CHIPS, 8, 256), f32),
+            pltpu.VMEM((CHIPS - 1, 8, 256), f32),
+            pltpu.VMEM((8, 256), f32),
+            pltpu.VMEM((2 * RANK, width), f32),
+            pltpu.VMEM((2, PLANE, 8, HD), f32),
+            pltpu.VMEM((PLANE, 8, HD), f32),
+            pltpu.VMEM((PLANE, 8, HD), f32),
+            pltpu.VMEM((PLANE - 1, 8, HD), f32),
+            pltpu.VMEM((8, HD), f32),
+            pltpu.VMEM((2, 8, PLANE * HD), f32),
+            dma((8,)),
+            dma((heads,)),
+            dma((heads,)),
+            dma((heads, 3)),
+            dma((heads, 3)),
+            dma((heads, 3)),
+            dma((heads, 3)),
+            dma((3,)),
+            dma((3,)),
+            dma((4,)),
+            dma((4,)),
+            dma((4,)),
+            dma((4,)),
+        ],
+        compiler_params=pltpu.CompilerParams(
+            dimension_semantics=("arbitrary",),
+            collective_id=2,
+            has_side_effects=True,
+            vmem_limit_bytes=48 << 20,
+        ),
+        cost_estimate=pl.CostEstimate(
+            flops=10 * heads * seq * seq * HD,
+            bytes_accessed=16 * seq * heads * HD,
+            transcendentals=heads * seq * seq,
+        ),
+        name="attention_step",
+    )(projected, projected, projected, down, qup, vup, cos, sin, out_grad, normed)
+
+
 def local(tokens, norm_gain, w_qkv, a_query, query_up_adapter, a_value, value_up_adapter, out_grad):
     projected, normed, down = gather_project(
         tokens[0], norm_gain, w_qkv, jnp.concatenate([a_query.T, a_value.T], 0)
     )
-    seq = projected.shape[0]
-    grad_rows = lax.all_to_all(out_grad[0], "tensor", split_axis=1, concat_axis=0, tiled=True)
-    cos, sin = rotary_tables(seq)
-    attended, gbq, gbv, mid_t = attention(
-        projected, down, down.T, query_up_adapter, value_up_adapter, cos, sin, grad_rows
+    cos, sin = rotary_tables(projected.shape[0])
+    out_rows, ga_query, ga_value, gb_query, gb_value = attention(
+        projected, down, query_up_adapter, value_up_adapter, cos, sin, out_grad[0], normed
     )
-    out_rows = lax.all_to_all(attended, "tensor", split_axis=0, concat_axis=1, tiled=True)
-    groups = lax.axis_size("tensor")
-    own = seq // groups
-    mid_split = mid_t.reshape(2 * RANK, groups, own).transpose(1, 0, 2)
-    mid = (
-        lax.all_to_all(mid_split, "tensor", split_axis=0, concat_axis=0, tiled=True)
-        .sum(axis=0)
-        .astype(jnp.bfloat16)
-    )
-    grad_a = ADAPTER_SCALE * jnp.einsum("rp,cpw->rcw", mid, normed, preferred_element_type=jnp.float32)
-    grad_a = grad_a.reshape(2 * RANK, -1)
-    up = jnp.concatenate([gbq, gbv], 1)
-    slots = jnp.zeros((groups, *up.shape), jnp.float32)
-    slots = lax.dynamic_update_index_in_dim(slots, up, lax.axis_index("tensor"), 0)
-    grad_a, slots = lax.psum((grad_a, slots), ALL)
-    up = lax.dynamic_index_in_dim(slots, lax.axis_index("tensor"), 0, keepdims=False)
-    return (
-        out_rows[None],
-        grad_a[:RANK].T,
-        up[:, : gbq.shape[1]],
-        grad_a[RANK:].T,
-        up[:, gbq.shape[1] :],
-    )
+    return out_rows[None], ga_query.T, gb_query, ga_value.T, gb_value
 
 
 def solution(mesh):

time: 357 us -> 196 us (0.55)
  waiting for transfers between devices: 154 us -> 0 us
  Pallas kernels: 152 us -> 189 us
  between operations: 14.1 us -> 0.71 us
  local copies, waits for them, and re-layouts: 18 us -> 4.9 us
  starting transfers between devices: 12.7 us -> 0 us
    psum x1 -> x0, waiting for transfers between devices: 150 us -> none  [local(): grad_a, slots = lax.psum((grad_a, slots), ALL)]
    pallas_call x1, Pallas kernels: 26.4 us -> 71 us  [attention(): pl.pallas_call(functools.partial(attention_kernel, seq), grid=(heads,), i...]
    all_to_all x3 -> x0, starting transfers between devices: 12.6 us -> none  [the longest x1 5.13 us: local(): lax.all_to_all(out_grad[0], 'tensor', split_axis=1, concat_axis=0, tiled=...]
    pallas_call x1, Pallas kernels: 125 us -> 118 us  [gather_project(): pl.pallas_call(functools.partial(project_kernel, rows), in_specs=[anywher...]
    all_to_all x3 -> x0, local copies, waits for them, and re-layouts: 5.71 us -> none  [the longest x2 4.49 us: local(): lax.all_to_all(out_grad[0], 'tensor', split_axis=1, concat_axis=0, tiled=...]
    all_to_all x3 -> x0, waiting for transfers between devices: 3.94 us -> none  [the longest x1 3.93 us: local(): lax.all_to_all(mid_split, 'tensor', split_axis=0, concat_axis=0, tiled=True)]
    unnamed x10 -> x17, local copies, waits for them, and re-layouts: 1.16 us -> 4.9 us
  transfers between devices with their start and end apart: 4 -> 0, of which waited for: 2 -> 0; matrix products, arithmetic and copies ran while one was open for 3% -> 0% of each run, Pallas kernels for 35% -> 0%
where the time goes in v3:
time: 196 us
  Pallas kernels  189 us (96%)
  local copies, waits for them, and re-layouts  4.9 us (3%)
    pallas_call x1, Pallas kernels, gather_project(): pl.pallas_call(functools.partial(project_kernel, rows), in_specs=[anywher...  118 us
    pallas_call x1, Pallas kernels, attention(): pl.pallas_call(functools.partial(attention_kernel, seq), grid=(heads,), i...  71 us
    unnamed x17, local copies, waits for them, and re-layouts  4.9 us

profile of v3, /device:TPU:1, one launch (start us, length us, event | category | flops | bytes accessed | tf_op | source)
XLA Modules:
  0.0 196.0 jit_solution(4709636049549503539)
XLA Ops:
  0.6 1.9 pad_maximum_fusion.adapt_ref
  2.5 0.0 copy-start
  2.5 0.0 copy-start.1
  2.5 0.0 copy-start.2
  2.5 0.0 copy-start.3
  2.5 0.0 copy-start.4
  2.5 117.6 %gather_project.1 = (f32[768,1280]{1,0:T(8,128)}, bf16[8,192,1024]{2,1,0:T(8,128)(2,1)}, bf16[768,32]{1,0:T(8,128)(2,1)}) custom-call(bf16[192,8192]{1,0:T(8,128)(2,1)} %bitcast.14, f32[1,8192]{1,0:T(1,128)} %bitcast.15, bf16[256,1280]{1,0:T(8,128)(2,1)} %w_hbm.1, bf16[32,8192]{1,0:T(8,128)(2,1)} %pad_maximum_fusion.adapt_ref), custom_call_target="tpu_custom_call" | custom-call | flops 16106127360 | bytes 20000000 | tf_op jit(solution)/shard_map/gather_project/pallas_call | solution.py:365
  120.1 0.0 copy-done
  120.1 0.0 copy-done.1
  120.2 0.0 copy-done.2
  120.2 0.0 copy-done.3
  120.2 0.0 copy-done.4
  120.2 0.0 copy-start.5
  120.2 0.9 copy-done.5
  121.1 71.0 %attention_step.1 = (bf16[192,4096]{1,0:T(8,128)(2,1)S(1)}, f32[16,8192]{1,0:T(8,128)S(1)}, f32[16,8192]{1,0:T(8,128)S(1)}, f32[16,1024]{1,0:T(8,128)S(1)}, f32[16,128]{1,0:T(8,128)S(1)}) custom-call(f32[768,1280]{1,0:T(8,128)} %get-tuple-element.13.proj_ref.key_ref.value_ref, f32[768,1280]{1,0:T(8,128)} %get-tuple-element.13.proj_ref.key_ref.value_ref, ...), custom_call_target="tpu_custom_call" | custom-call | flops 6039797760 | bytes 12582912 | tf_op jit(solution)/shard_map/attention_step/pallas_call | solution.py:801
  192.1 1.1 copy.20
  193.2 0.8 copy.21
  194.0 0.6 copy.22
  194.7 0.8 copy.23
  195.4 0.6 copy.24
Async XLA Ops:
  2.5 117.7 %copy-start = (bf16[1,192,4096]{2,1,0:T(8,128)(2,1)S(1)}, bf16[1,192,4096]{2,1,0:T(8,128)(2,1)}, u32[]{:S(2)}) copy-start(bf16[1,192,4096]{2,1,0:T(8,128)(2,1)} %param.17) | copy-start | bytes 4718596
  2.5 117.7 %copy-start.1 = (bf16[16,1024]{1,0:T(8,128)(2,1)S(1)}, bf16[16,1024]{1,0:T(8,128)(2,1)}, u32[]{:S(2)}) copy-start(bf16[16,1024]{1,0:T(8,128)(2,1)} %qup_ref.1) | copy-start | bytes 98308
  2.5 117.7 %copy-start.2 = (bf16[16,128]{1,0:T(8,128)(2,1)S(1)}, bf16[16,128]{1,0:T(8,128)(2,1)}, u32[]{:S(2)}) copy-start(bf16[16,128]{1,0:T(8,128)(2,1)} %vup_ref.1) | copy-start | bytes 12292
  2.5 117.7 %copy-start.3 = (f32[768,128]{1,0:T(8,128)S(1)}, f32[768,128]{1,0:T(8,128)}, u32[]{:S(2)}) copy-start(f32[768,128]{1,0:T(8,128)} %constant.5.clone.sin_ref) | copy-start | bytes 1179652
  2.5 117.7 %copy-start.4 = (f32[768,128]{1,0:T(8,128)S(1)}, f32[768,128]{1,0:T(8,128)}, u32[]{:S(2)}) copy-start(f32[768,128]{1,0:T(8,128)} %constant.4.clone.cos_ref) | copy-start | bytes 1179652
  120.2 0.9 copy-start.5

commit v4 on v2

v4 whole, which is shorter than its diff:
```python
import functools
import math

import jax
import jax.numpy as jnp
import numpy as np
from jax import lax
from jax.experimental import pallas as pl
from jax.experimental.pallas import tpu as pltpu
from jax.sharding import PartitionSpec as P

HD = 128
QUERY_PER_KV = 8
RANK = 16
QB = 256

EPSILON = 1e-05
ADAPTER_SCALE = 2.0
ROPE_BASE = 500000.0
SCORE_SCALE = 1.0 / math.sqrt(HD)
LOG2E = 1.4426950408889634


def rotary_tables(sequence_length):
    half_dim = HD // 2
    inv_freq = ROPE_BASE ** (-np.arange(half_dim) / half_dim)
    angles = np.arange(sequence_length)[:, None] * inv_freq
    cosine, sine = np.cos(angles), np.sin(angles)
    return (
        np.concatenate([cosine, cosine], 1).astype(np.float32),
        np.concatenate([-sine, sine], 1).astype(np.float32),
    )


def dot_nt(a, b):
    return lax.dot_general(a, b, (((1,), (1,)), ((), ())), preferred_element_type=jnp.float32)


def dot_nn(a, b):
    return jnp.dot(a, b, preferred_element_type=jnp.float32)


def rotate(x, cos, sin):
    return x * cos + pltpu.roll(x, HD // 2, 1) * sin


MESH = pl.DeviceIdType.MESH
CHUNKS = 8
OFFSETS = (0, 3, 1, 2)


class Place:
    def __init__(self):
        self.dp = lax.axis_index("dp")
        self.fs = lax.axis_index("fsdp")
        self.y = lax.axis_index("tensor")
        self.core = lax.rem(self.dp, 2)
        self.x = lax.div(self.dp, 2) * 2 + lax.rem(self.fs, 2)
        self.z = lax.div(self.fs, 2)

    def ring(self, core):
        first = self.x * (1 - core) + self.z * core
        second = self.z * (1 - core) + self.x * core
        return first, second

    def plane(self, core, a, b):
        first, second = self.ring(core)
        first = lax.rem(first + a, 4)
        second = lax.rem(second + b, 4)
        x = first * (1 - core) + second * core
        z = second * (1 - core) + first * core
        return lax.div(x, 2) * 2 + core, z * 2 + lax.rem(x, 2)

    def near(self, a, b):
        return (*self.plane(self.core, a, b), self.y)

    def along(self, c):
        return (self.dp, self.fs, lax.rem(self.y + c, 4))

    def partner(self):
        return (self.dp + 1 - 2 * self.core, self.fs, self.y)


CHIPS = 64
PLANE = 16
LAG = 2


def step_kernel(
    rows,
    tok_hbm,
    gain_hbm,
    w_hbm,
    aq_hbm,
    av_hbm,
    qup_hbm,
    vup_hbm,
    cos_hbm,
    sin_hbm,
    grad_hbm,
    out_hbm,
    ga_q_hbm,
    ga_v_hbm,
    gb_q_hbm,
    gb_v_hbm,
    raw,
    scale_scr,
    x_buf,
    w_buf,
    acc,
    down_scr,
    gain_ref,
    adapt_ref,
    qup_ref,
    vup_ref,
    cos_ref,
    sin_ref,
    stage,
    q_buf,
    k_scr,
    v_scr,
    down_b,
    down_t,
    dv_scr,
    dq_scr,
    mid_scr,
    mid_recv,
    mid_all,
    g_buf,
    o_buf,
    part,
    part_recv,
    up_part,
    up_recv,
    total,
    rs_recv,
    final,
    up_final,
    res,
    up_res,
    ag_size,
    tok_sem,
    load_sem,
    own_sem,
    w_send,
    w_recv,
    d_send,
    d_recv,
    x_send,
    x_recv,
    own_g_sem,
    o_own_sem,
    g_send,
    g_recv,
    o_send,
    o_recv,
    m_send,
    m_recv,
    c_send,
    c_recv,
    r_send,
    r_recv,
    write_sem,
):
    heads = QUERY_PER_KV
    group = heads * HD
    seq = 4 * rows
    blocks = seq // QB

    me = Place()
    shard = w_hbm.shape[0]
    half_shard = shard // 2
    width = tok_hbm.shape[1]
    wide = width // CHUNKS
    cols = w_hbm.shape[1]
    parts = tok_sem.shape[0]
    span = rows // parts

    def tok_copy(i):
        piece = pl.ds(i * span, span)
        return pltpu.make_async_copy(tok_hbm.at[piece], raw.at[piece], tok_sem.at[i])

    for i in range(parts):
        tok_copy(i).start()

    loads = [
        pltpu.make_async_copy(src, dst, load_sem.at[i])
        for i, (src, dst) in enumerate(
            (
                (gain_hbm, gain_ref),
                (aq_hbm, adapt_ref.at[pl.ds(0, RANK)]),
                (av_hbm, adapt_ref.at[pl.ds(RANK, RANK)]),
                (qup_hbm, qup_ref),
                (vup_hbm, vup_ref),
                (cos_hbm, cos_ref),
                (sin_hbm, sin_ref),
                (grad_hbm, stage),
            )
        )
    ]

    def block(core, a, b):
        dp, fs = me.plane(core, a, b)
        return pl.multiple_of((dp * 8 + fs) * shard, shard)

    own = block(me.core, 0, 0)
    own_copy = pltpu.make_async_copy(w_hbm, w_buf.at[pl.ds(own, shard)], own_sem)
    own_copy.start()

    plane = lax.div(me.dp, 2) * 8 + me.fs
    chip = plane * 4 + me.y

    def of_chip(index):
        at = lax.div(index, 4)
        return (lax.div(at, 8) * 2 + me.core, lax.rem(at, 8), lax.rem(index, 4))

    barrier = pltpu.get_barrier_semaphore()

    @pl.loop(1, CHIPS)
    def _(o):
        pl.semaphore_signal(
            barrier, inc=1, device_id=of_chip(lax.rem(chip + o, CHIPS)), device_id_type=MESH
        )

    pl.semaphore_signal(barrier, inc=1, device_id=me.partner(), device_id_type=MESH)
    for load in loads:
        load.start()

    def lines_of(block):
        return pl.ds(pl.multiple_of(block * rows, rows), rows)

    def columns(block, h):
        return pl.ds(pl.multiple_of(block * group + h * HD, HD), HD)

    def remote(src, dst, send, recv, device):
        return pltpu.make_async_remote_copy(
            src_ref=src,
            dst_ref=dst,
            send_sem=send,
            recv_sem=recv,
            device_id=device,
            device_id_type=MESH,
        )

    def own_grad(h):
        return pltpu.make_async_copy(
            grad_hbm.at[:, columns(me.y, h)], g_buf.at[h, lines_of(me.y)], own_g_sem.at[h]
        )

    def grad_copy(h, c):
        to = lax.rem(me.y + c, 4)
        return remote(
            stage.at[:, columns(to, h)],
            g_buf.at[h, lines_of(me.y)],
            g_send.at[h, c - 1],
            g_recv.at[h, c - 1],
            me.along(c),
        )

    def grad_arrival(h, c):
        ref = g_buf.at[h, lines_of(lax.rem(me.y + 4 - c, 4))]
        return remote(ref, ref, g_send.at[h, c - 1], g_recv.at[h, c - 1], me.along(c))

    def own_out(h):
        return pltpu.make_async_copy(
            o_buf.at[h, lines_of(me.y)], out_hbm.at[:, columns(me.y, h)], o_own_sem.at[h]
        )

    def out_copy(h, c):
        to = lax.rem(me.y + c, 4)
        return remote(
            o_buf.at[h, lines_of(to)],
            out_hbm.at[:, columns(me.y, h)],
            o_send.at[h, c - 1],
            o_recv.at[h, c - 1],
            me.along(c),
        )

    def out_arrival(h, c):
        ref = out_hbm.at[:, columns(lax.rem(me.y + 4 - c, 4), h)]
        return remote(ref, ref, o_send.at[h, c - 1], o_recv.at[h, c - 1], me.along(c))

    sends = []

    def w_copy(a, b, device, kind, way, piece=None, source=None):
        start = block(me.core, a, b)
        size = shard
        if piece is not None:
            start, size = pl.multiple_of(start + piece * half_shard, half_shard), half_shard
        dst = w_buf.at[pl.ds(start, size)]
        return pltpu.make_async_remote_copy(
            src_ref=dst if source is None else source,
            dst_ref=dst,
            send_sem=w_send.at[kind, way],
            recv_sem=w_recv.at[kind, way],
            device_id=device,
            device_id_type=MESH,
        )

    def w_start(*args, **kwargs):
        copy = w_copy(*args, **kwargs)
        copy.start()
        sends.append(copy)

    def d_copy(core, event, a, b, source=None):
        dst = w_buf.at[pl.ds(block(core, a, b), shard)]
        return pltpu.make_async_remote_copy(
            src_ref=dst if source is None else source,
            dst_ref=dst,
            send_sem=d_send.at[event],
            recv_sem=d_recv.at[event],
            device_id=me.partner(),
            device_id_type=MESH,
        )

    order = []

    def share(a, b, source=None):
        copy = d_copy(me.core, len(order), a, b, source)
        copy.start()
        sends.append(copy)
        order.append((a, b))

    for i in range(parts):
        tok_copy(i).wait()

        @pl.loop(0, span // 16)
        def _(r):
            piece = pl.ds(pl.multiple_of(i * span + r * 16, 16), 16)
            squares = jnp.zeros((16, wide), jnp.float32)
            for c in range(CHUNKS):
                value = raw[piece, c * wide : (c + 1) * wide].astype(jnp.float32)
                squares = squares + value * value
            mean = jnp.sum(squares, axis=-1, keepdims=True) * (1.0 / width)
            scale_scr[piece, :] = jnp.broadcast_to(lax.rsqrt(mean + EPSILON), (16, 128))

    def x_copy(row_block, chunk, device, way):
        ref = x_buf.at[row_block, chunk]
        return pltpu.make_async_remote_copy(
            src_ref=ref,
            dst_ref=ref,
            send_sem=x_send.at[way, chunk],
            recv_sem=x_recv.at[way // 2 * 2 if way > 1 else way, chunk],
            device_id=device,
            device_id_type=MESH,
        )

    def normalize_chunk(c):
        @pl.loop(0, rows // 16)
        def _(r):
            piece = pl.ds(pl.multiple_of(r * 16, 16), 16)
            scale = scale_scr[piece, :]
            for k in range(wide // 128):
                lanes = slice(c * wide + k * 128, c * wide + (k + 1) * 128)
                value = raw[piece, lanes].astype(jnp.float32)
                x_buf[me.y, c, piece, k * 128 : (k + 1) * 128] = (
                    value * scale * gain_ref[:, lanes]
                ).astype(jnp.bfloat16)

    def x_start(row_block, chunk, device, way):
        copy = x_copy(row_block, chunk, device, way)
        copy.start()
        sends.append(copy)

    middle = CHUNKS // 2
    loads[0].wait()
    normalize_chunk(0)
    normalize_chunk(middle)
    pl.semaphore_wait(barrier, CHIPS)

    w_start(0, 0, me.near(1, 0), 4, 0, source=w_hbm)
    w_start(0, 0, me.near(3, 0), 4, 1, source=w_hbm)
    w_start(0, 0, me.near(0, 1), 0, 0, source=w_hbm)
    w_start(0, 0, me.near(0, 3), 0, 1, source=w_hbm)
    share(0, 0, source=w_hbm)

    for c in range(middle):
        x_start(me.y, c, me.along(1), 0)
        x_start(me.y, c + middle, me.along(3), 1)
        if c + 1 < middle:
            normalize_chunk(c + 1)
            normalize_chunk(c + 1 + middle)
    for c in range(middle):
        x_start(me.y, c + middle, me.along(1), 0)
        x_start(me.y, c, me.along(3), 1)

    acc[...] = jnp.zeros_like(acc)
    down_scr[...] = jnp.zeros_like(down_scr)

    dv_scr[...] = jnp.zeros_like(dv_scr)
    mid_scr[...] = jnp.zeros_like(mid_scr)
    up_part[...] = jnp.zeros_like(up_part)
    for load in loads[1:]:
        load.wait()

    def arrived(a, b, kind, way, piece=None):
        w_copy(a, b, me.near(0, 1), kind, way, piece).wait_recv()

    def spread(a, kind):
        w_start(a, 0, me.near(0, 1), kind, 0)
        w_start(a, 0, me.near(0, 3), kind, 1)

    own_copy.wait()
    arrived(3, 0, 4, 0)
    w_start(3, 0, me.near(1, 0), 4, 2, piece=0)
    spread(3, 1)
    share(3, 0)
    arrived(1, 0, 4, 1)
    w_start(1, 0, me.near(3, 0), 4, 3, piece=1)
    spread(1, 2)
    share(1, 0)
    for kind, a in enumerate(OFFSETS):
        if kind == 3:
            arrived(2, 0, 4, 2, piece=0)
            arrived(2, 0, 4, 3, piece=1)
            spread(2, 3)
            share(2, 0)
        arrived(a, 3, kind, 0)
        w_start(a, 3, me.near(0, 1), kind, 2, piece=0)
        share(a, 3)
        arrived(a, 1, kind, 1)
        w_start(a, 1, me.near(0, 3), kind, 3, piece=1)
        share(a, 1)
        if kind > 0:
            before = OFFSETS[kind - 1]
            arrived(before, 2, kind - 1, 2, piece=0)
            arrived(before, 2, kind - 1, 3, piece=1)
            share(before, 2)
    arrived(OFFSETS[3], 2, 3, 2, piece=0)
    arrived(OFFSETS[3], 2, 3, 3, piece=1)
    share(OFFSETS[3], 2)

    minus = lax.rem(me.y + 3, 4)
    plus = lax.rem(me.y + 1, 4)
    far = lax.rem(me.y + 2, 4)
    for c in range(middle):
        x_copy(minus, c, me.along(1), 0).wait_recv()
        x_start(minus, c, me.along(1), 2)
        x_copy(plus, c + middle, me.along(1), 1).wait_recv()
        x_start(plus, c + middle, me.along(3), 2)

    @pl.loop(0, heads)
    def _(h):
        own_grad(h).start()
        for c in (1, 3, 2):
            grad_copy(h, c).start()

    for event, (a, b) in enumerate(order):
        d_copy(1 - me.core, event, a, b).wait_recv()

    def multiply(row_block, chunk):
        value = x_buf[row_block, chunk]
        lines = pl.ds(pl.multiple_of(row_block * rows, rows), rows)
        depth = pl.ds(pl.multiple_of(chunk * wide, wide), wide)
        for n in range(cols // 256):
            lanes = slice(n * 256, (n + 1) * 256)
            acc[lines, lanes] += dot_nn(value, w_buf[depth, lanes])
        down_scr[lines, :] += dot_nt(value, adapt_ref[:, depth])

    def prepare(row_block):
        lines = pl.ds(pl.multiple_of(row_block * rows, rows), rows)
        down = down_scr[lines, :].astype(jnp.bfloat16)
        down_b[lines, :] = down
        cos, sin = cos_ref[lines, :], sin_ref[lines, :]
        for h in range(heads):
            lanes = slice(h * HD, (h + 1) * HD)
            value = acc[lines, lanes] + ADAPTER_SCALE * dot_nn(down[:, :RANK], qup_ref[:, lanes])
            value = value.astype(jnp.bfloat16).astype(jnp.float32)
            q_buf[h, lines, :] = rotate(value, cos, sin).astype(jnp.bfloat16)
        value = acc[lines, group : group + HD].astype(jnp.bfloat16).astype(jnp.float32)
        k_scr[lines, :] = rotate(value, cos, sin).astype(jnp.bfloat16)
        v_scr[lines, :] = (
            acc[lines, group + HD :] + ADAPTER_SCALE * dot_nn(down[:, RANK:], vup_ref[...])
        ).astype(jnp.bfloat16)

    @pl.loop(0, CHUNKS)
    def _(c):
        multiply(me.y, c)

    @pl.loop(0, CHUNKS)
    def _(c):
        @pl.when(c >= middle)
        def _():
            x_copy(minus, c, me.along(1), 0).wait_recv()

        multiply(minus, c)

    @pl.loop(0, CHUNKS)
    def _(c):
        @pl.when(c < middle)
        def _():
            x_copy(plus, c, me.along(1), 1).wait_recv()

        multiply(plus, c)

    @pl.loop(0, 3)
    def _(c):
        prepare(lax.rem(me.y + 3 + c, 4))

    @pl.loop(0, middle)
    def _(c):
        x_copy(far, c, me.along(1), 2).wait_recv()
        multiply(far, c)
        x_copy(far, c + middle, me.along(1), 2).wait_recv()
        multiply(far, c + middle)

    prepare(far)
    down_t[...] = down_b[...].astype(jnp.float32).T.astype(jnp.bfloat16)

    row = lax.broadcasted_iota(jnp.int32, (QB, QB), 0)
    col = lax.broadcasted_iota(jnp.int32, (QB, QB), 1)
    causal = row >= col
    factor = SCORE_SCALE * LOG2E

    def send_out(h):
        own_out(h).start()
        for c in (1, 3, 2):
            out_copy(h, c).start()

    @pl.loop(0, heads)
    def _(head):
        own_grad(head).wait()
        for c in (1, 3, 2):
            grad_arrival(head, c).wait_recv()

        for i in range(blocks):
            own_rows = slice(i * QB, (i + 1) * QB)
            q = q_buf[head, own_rows, :]
            grad = g_buf[head, own_rows, :]
            grad_t = grad.T
            scores = []
            for j in range(i + 1):
                s = dot_nt(q, k_scr[j * QB : (j + 1) * QB, :])
                if j == i:
                    s = jnp.where(causal, s, -1e30)
                scores.append(s)
            top = functools.reduce(jnp.maximum, scores)
            top = jnp.max(top, axis=-1, keepdims=True) * factor
            weights = [jnp.exp2(s * factor - top) for s in scores]
            whole = jnp.sum(functools.reduce(jnp.add, weights), axis=-1, keepdims=True)
            inverse = 1.0 / whole
            probs = [w * inverse for w in weights]
            rounded = [p.astype(jnp.bfloat16) for p in probs]
            attended = functools.reduce(
                jnp.add, [dot_nn(rounded[j], v_scr[j * QB : (j + 1) * QB, :]) for j in range(i + 1)]
            )
            o_buf[head, own_rows, :] = attended.astype(jnp.bfloat16)
            prods = []
            for j in range(i + 1):
                keys = slice(j * QB, (j + 1) * QB)
                dp = dot_nt(grad, v_scr[keys, :])
                prods.append(probs[j] * dp)
                dv_scr[:, keys] += dot_nn(grad_t, rounded[j])
            inner = jnp.sum(functools.reduce(jnp.add, prods), axis=-1, keepdims=True)
            ds = [(prods[j] - probs[j] * inner).astype(jnp.bfloat16) for j in range(i + 1)]
            dq = functools.reduce(
                jnp.add, [dot_nn(ds[j], k_scr[j * QB : (j + 1) * QB, :]) for j in range(i + 1)]
            )
            dq = (dq * SCORE_SCALE).astype(jnp.bfloat16).astype(jnp.float32)
            dq_scr[own_rows, :] = rotate(dq, cos_ref[own_rows, :], -sin_ref[own_rows, :]).astype(
                jnp.bfloat16
            )


        @pl.when(head >= LAG)
        def _():
            send_out(head - LAG)

        up = dot_nn(down_t[:RANK, :], dq_scr[...])
        up_part[0, head, :, :HD] = up[:8]
        up_part[1, head, :, :HD] = up[8:]
        lanes = pl.ds(pl.multiple_of(head * HD, HD), HD)
        for b in range(4):
            mid_scr[b, :RANK, :] += dot_nt(qup_ref[:, lanes], dq_scr[b * rows : (b + 1) * rows, :])

    dv = dv_scr[...].T.astype(jnp.bfloat16)
    for b in range(4):
        mid_scr[b, RANK:, :] = dot_nt(vup_ref[...], dv[b * rows : (b + 1) * rows])
    up = dot_nn(down_t[RANK:, :], dv)
    up_part[0, heads, :, :HD] = up[:8]
    up_part[1, heads, :, :HD] = up[8:]

    def mid_copy(c):
        return remote(
            mid_scr.at[lax.rem(me.y + c, 4)],
            mid_recv.at[c - 1],
            m_send.at[c - 1],
            m_recv.at[c - 1],
            me.along(c),
        )

    def mid_share(c):
        return remote(
            mid_all.at[me.y], mid_all.at[me.y], m_send.at[2 + c], m_recv.at[2 + c], me.along(c)
        )

    def mid_other(c):
        ref = mid_all.at[lax.rem(me.y + 4 - c, 4)]
        return remote(ref, ref, m_send.at[2 + c], m_recv.at[2 + c], me.along(c))

    for c in (1, 3, 2):
        mid_copy(c).start()
    for c in (1, 3, 2):
        mid_copy(c).wait_recv()
    mid_all[me.y] = (mid_scr[me.y] + mid_recv[0] + mid_recv[1] + mid_recv[2]).astype(jnp.bfloat16)
    for c in (1, 3, 2):
        mid_share(c).start()

    @pl.loop(heads - LAG, heads)
    def _(h):
        send_out(h)

    for c in (1, 3, 2):
        mid_other(c).wait_recv()

    def partial(half):
        made = dot_nn(mid_all[0], x_buf[0, 2 * me.y + half])
        for b in range(1, 4):
            made += dot_nn(mid_all[b], x_buf[b, 2 * me.y + half])
        for r in range(4):
            for k in range(4):
                part[half, r * 4 + k] = made[r * 8 : (r + 1) * 8, k * 256 : (k + 1) * 256]

    partial(1 - me.core)
    swap = remote(part.at[1 - me.core], part_recv, c_send.at[0], c_recv.at[0], me.partner())
    up_swap = remote(up_part.at[1 - me.core], up_recv, c_send.at[1], c_recv.at[1], me.partner())
    swap.start()
    up_swap.start()
    partial(me.core)
    up_swap.wait_recv()
    swap.wait_recv()
    total[:, :, :256] = part[me.core] + part_recv[...]
    total[:, :, 256:] = up_part[me.core] + up_recv[...]

    @pl.loop(1, PLANE)
    def _(o):
        to = lax.rem(plane + o, PLANE)
        remote(
            total.at[to], rs_recv.at[o - 1], r_send.at[0], r_recv.at[0], of_chip(to * 4 + me.y)
        ).start()

    many = remote(rs_recv, rs_recv, r_send.at[0], r_recv.at[0], me.partner())
    many.wait_recv()
    summed = total[plane]
    for o in range(PLANE - 1):
        summed += rs_recv[o]
    summed = ADAPTER_SCALE * summed
    final[...] = summed[:, :256]
    up_final[...] = summed[:, 256:]

    at_rows = pl.ds(pl.multiple_of(lax.div(plane, 4) * 8, 8), 8)
    at_cols = pl.ds(pl.multiple_of(lax.rem(plane, 4) * 256, 256), 256)
    up_cols = pl.ds(pl.multiple_of(plane * HD, HD), HD)

    @pl.loop(1, CHIPS)
    def _(o):
        to = lax.rem(chip + o, CHIPS)
        remote(
            final,
            res.at[me.core, me.y, at_rows, at_cols],
            r_send.at[1],
            r_recv.at[1],
            of_chip(to),
        ).start()

    @pl.loop(1, PLANE)
    def _(o):
        to = lax.rem(plane + o, PLANE)
        remote(
            up_final,
            up_res.at[me.core, :, up_cols],
            r_send.at[2],
            r_recv.at[2],
            of_chip(to * 4 + me.y),
        ).start()

    res[me.core, me.y, at_rows, at_cols] = final[...]
    up_res[me.core, :, up_cols] = up_final[...]
    all_of = remote(ag_size, ag_size, r_send.at[1], r_recv.at[1], me.partner())
    up_size = part_recv.at[pl.ds(0, PLANE - 1), :, pl.ds(0, HD)]
    up_all = remote(up_size, up_size, r_send.at[2], r_recv.at[2], me.partner())
    up_all.wait_recv()
    up_half = remote(
        up_res.at[me.core], up_res.at[me.core], c_send.at[2], c_recv.at[2], me.partner()
    )
    up_half.start()
    all_of.wait_recv()
    half = remote(res.at[me.core], res.at[me.core], c_send.at[3], c_recv.at[3], me.partner())
    half.start()

    def grad_a_writes(b, first):
        copies = []
        for yy in range(4):
            cols_out = pl.ds(pl.multiple_of(yy * 2048 + b * 1024, 1024), 1024)
            for i, dst in enumerate((ga_q_hbm, ga_v_hbm)):
                copies.append(
                    pltpu.make_async_copy(
                        res.at[b, yy, pl.ds(i * RANK, RANK)],
                        dst.at[:, cols_out],
                        write_sem.at[first + yy * 2 + i],
                    )
                )
        return copies

    def grad_b_writes(b, first):
        eight = pl.ds(pl.multiple_of(b * 8, 8), 8)
        return [
            pltpu.make_async_copy(
                up_res.at[b, :, pl.ds(0, group)], gb_q_hbm.at[eight], write_sem.at[first]
            ),
            pltpu.make_async_copy(
                up_res.at[b, :, pl.ds(group, HD)], gb_v_hbm.at[eight], write_sem.at[first + 1]
            ),
        ]

    writes = grad_a_writes(me.core, 0) + grad_b_writes(me.core, 8)
    for copy in writes:
        copy.start()
    @pl.loop(0, heads)
    def _(h):
        own_out(h).wait()
        for c in (1, 3, 2):
            grad_copy(h, c).wait_send()
            out_copy(h, c).wait_send()
            out_arrival(h, c).wait_recv()

    for copy in sends:
        copy.wait_send()
    up_other = up_res.at[1 - me.core]
    remote(up_other, up_other, c_send.at[2], c_recv.at[2], me.partner()).wait_recv()
    other = res.at[1 - me.core]
    remote(other, other, c_send.at[3], c_recv.at[3], me.partner()).wait_recv()
    late = grad_a_writes(1 - me.core, 10) + grad_b_writes(1 - me.core, 18)
    for copy in late:
        copy.start()
    for c in (1, 3, 2):
        mid_copy(c).wait_send()
        mid_share(c).wait_send()
    for copy in (up_swap, swap, many, all_of, up_all, up_half, half):
        copy.wait_send()
    for copy in writes + late:
        copy.wait()


def fused_step(tokens, gain, w_qkv, aq_t, av_t, qup, vup, cos, sin, out_grad):
    rows, width = tokens.shape
    shard, cols = w_qkv.shape
    heads = QUERY_PER_KV
    seq = 4 * rows
    wide = width // CHUNKS
    anywhere = pl.BlockSpec(memory_space=pl.ANY)
    dma = pltpu.SemaphoreType.DMA
    f32, bf16 = jnp.float32, jnp.bfloat16
    return pl.pallas_call(
        functools.partial(step_kernel, rows),
        in_specs=[anywhere] * 10,
        out_specs=[anywhere] * 5,
        out_shape=[
            jax.ShapeDtypeStruct((rows, 4 * heads * HD), bf16),
            jax.ShapeDtypeStruct((RANK, width), f32),
            jax.ShapeDtypeStruct((RANK, width), f32),
            jax.ShapeDtypeStruct((RANK, heads * HD), f32),
            jax.ShapeDtypeStruct((RANK, HD), f32),
        ],
        scratch_shapes=[
            pltpu.VMEM((rows, width), bf16),
            pltpu.VMEM((rows, 128), f32),
            pltpu.VMEM((4, CHUNKS, rows, wide), bf16),
            pltpu.VMEM((width, cols), bf16),
            pltpu.VMEM((seq, cols), f32),
            pltpu.VMEM((seq, 2 * RANK), f32),
            pltpu.VMEM((1, width), f32),
            pltpu.VMEM((2 * RANK, width), bf16),
            pltpu.VMEM((RANK, heads * HD), bf16),
            pltpu.VMEM((RANK, HD), bf16),
            pltpu.VMEM((seq, HD), f32),
            pltpu.VMEM((seq, HD), f32),
            pltpu.VMEM((rows, 4 * heads * HD), bf16),
            pltpu.VMEM((heads, seq, HD), bf16),
            pltpu.VMEM((seq, HD), bf16),
            pltpu.VMEM((seq, HD), bf16),
            pltpu.VMEM((seq, 2 * RANK), bf16),
            pltpu.VMEM((2 * RANK, seq), bf16),
            pltpu.VMEM((HD, seq), f32),
            pltpu.VMEM((seq, HD), bf16),
            pltpu.VMEM((4, 2 * RANK, rows), f32),
            pltpu.VMEM((3, 2 * RANK, rows), f32),
            pltpu.VMEM((4, 2 * RANK, rows), bf16),
            pltpu.VMEM((heads, seq, HD), bf16),
            pltpu.VMEM((heads, seq, HD), bf16),
            pltpu.VMEM((2, PLANE, 8, 256), f32),
            pltpu.VMEM((PLANE, 8, 256), f32),
            pltpu.VMEM((2, PLANE, 8, HD), f32),
            pltpu.VMEM((PLANE, 8, HD), f32),
            pltpu.VMEM((PLANE, 8, 256 + HD), f32),
            pltpu.VMEM((PLANE - 1, 8, 256 + HD), f32),
            pltpu.VMEM((8, 256), f32),
            pltpu.VMEM((8, HD), f32),
            pltpu.VMEM((2, 4, 2 * RANK, 1024), f32),
            pltpu.VMEM((2, 8, PLANE * HD), f32),
            pltpu.VMEM((CHIPS - 1, 8, 256), f32),
            dma((4,)),
            dma((8,)),
            dma(()),
            dma((5, 4)),
            dma((5, 4)),
            dma((16,)),
            dma((16,)),
            dma((3, CHUNKS)),
            dma((3, CHUNKS)),
            dma((heads,)),
            dma((heads,)),
            dma((heads, 3)),
            dma((heads, 3)),
            dma((heads, 3)),
            dma((heads, 3)),
            dma((6,)),
            dma((6,)),
            dma((4,)),
            dma((4,)),
            dma((3,)),
            dma((3,)),
            dma((20,)),
        ],
        compiler_params=pltpu.CompilerParams(
            collective_id=1, has_side_effects=True, vmem_limit_bytes=63 << 20
        ),
        cost_estimate=pl.CostEstimate(
            flops=2 * seq * width * cols,
            bytes_accessed=10 * 1000 * 1000,
            transcendentals=heads * seq * seq,
        ),
        name="fused_step",
    )(tokens, gain.reshape(1, width), w_qkv, aq_t, av_t, qup, vup, cos, sin, out_grad)


def local(tokens, norm_gain, w_qkv, a_query, query_up_adapter, a_value, value_up_adapter, out_grad):
    cos, sin = rotary_tables(4 * tokens.shape[1])
    out_rows, ga_query, ga_value, gb_query, gb_value = fused_step(
        tokens[0],
        norm_gain,
        w_qkv,
        a_query.T,
        a_value.T,
        query_up_adapter,
        value_up_adapter,
        cos,
        sin,
        out_grad[0],
    )
    return out_rows[None], ga_query.T, gb_query, ga_value.T, gb_value


def solution(mesh):
    return jax.shard_map(
        local,
        mesh=mesh,
        in_specs=(
            P(("dp", "fsdp"), "tensor", None),
            P(),
            P(("dp", "fsdp"), "tensor"),
            P(),
            P(None, "tensor"),
            P(),
            P(None, "tensor"),
            P(("dp", "fsdp"), "tensor", None),
        ),
        out_specs=(
            P(("dp", "fsdp"), "tensor", None),
            P(),
            P(None, "tensor"),
            P(),
            P(None, "tensor"),
        ),
        check_vma=False,
    )
```

time: 357 us -> 179 us (0.50)
  waiting for transfers between devices: 154 us -> 0 us
  Pallas kernels: 152 us -> 172 us
  between operations: 14.1 us -> 0.67 us
  starting transfers between devices: 12.7 us -> 0 us
  local copies, waits for them, and re-layouts: 18 us -> 5.62 us
  other arithmetic: 5.25 us -> 0 us
    psum x1 -> x0, waiting for transfers between devices: 150 us -> none  [local(): grad_a, slots = lax.psum((grad_a, slots), ALL)]
    pallas_call x2 -> x1, Pallas kernels: 152 us -> 172 us  [fused_step(): pl.pallas_call(functools.partial(step_kernel, rows), in_specs=[anywhere]...]
    all_to_all x3 -> x0, starting transfers between devices: 12.6 us -> none  [the longest x1 5.13 us: local(): lax.all_to_all(out_grad[0], 'tensor', split_axis=1, concat_axis=0, tiled=...]
    all_to_all x3 -> x0, local copies, waits for them, and re-layouts: 5.71 us -> none  [the longest x2 4.49 us: local(): lax.all_to_all(out_grad[0], 'tensor', split_axis=1, concat_axis=0, tiled=...]
    unnamed x10 -> x13, local copies, waits for them, and re-layouts: 1.16 us -> 5.62 us
    all_to_all x3 -> x0, waiting for transfers between devices: 3.94 us -> none  [the longest x1 3.93 us: local(): lax.all_to_all(mid_split, 'tensor', split_axis=0, concat_axis=0, tiled=True)]
  transfers between devices with their start and end apart: 4 -> 0, of which waited for: 2 -> 0; matrix products, arithmetic and copies ran while one was open for 3% -> 0% of each run, Pallas kernels for 35% -> 0%
where the time goes in v4:
time: 179 us
  Pallas kernels  172 us (96%)
  local copies, waits for them, and re-layouts  5.62 us (3%)
    pallas_call x1, Pallas kernels, fused_step(): pl.pallas_call(functools.partial(step_kernel, rows), in_specs=[anywhere]...  172 us
    unnamed x13, local copies, waits for them, and re-layouts  5.62 us

profile of v4, /device:TPU:1, one launch (start us, length us, event | category | flops | bytes accessed | tf_op | source)
XLA Modules:
  0.0 178.7 jit_solution(5897251423449417648)
XLA Ops:
  0.6 172.4 %fused_step.1 = (bf16[192,4096]{1,0:T(8,128)(2,1)}, f32[16,8192]{1,0:T(8,128)}, f32[16,8192]{1,0:T(8,128)}, f32[16,1024]{1,0:T(8,128)}, f32[16,128]{1,0:T(8,128)}) custom-call(bf16[192,8192]{1,0:T(8,128)(2,1)} %bitcast.11, f32[1,8192]{1,0:T(1,128)} %bitcast.15, bf16[256,1280]{1,0:T(8,128)(2,1)} %w_hbm.1, bf16[16,8192]{1,0:T(8,128)(2,1)} %bitcast.13, ...), custom_call_target="tpu_custom_call" | custom-call | flops 16106127360 | bytes 10000000 | tf_op jit(solution)/shard_map/fused_step/pallas_call | solution.py:754
  173.0 0.0 copy-start.1
  173.0 0.0 copy-start.2
  173.1 0.0 copy-start
  173.1 2.8 %copy.20 = bf16[1,192,4096]{2,1,0:T(8,128)(2,1)} copy(bf16[1,192,4096]{2,1,0:T(8,128)(2,1)} %bitcast.8) | data formatting | bytes 3145728
  175.9 0.0 copy-done.1
  175.9 0.0 copy-start.3
  175.9 0.8 copy.21
  176.7 0.0 copy-done.2
  176.7 0.6 copy.22
  177.3 0.0 copy-done
  177.3 0.8 copy.23
  178.1 0.0 copy-done.3
  178.1 0.6 copy.24
Async XLA Ops:
  173.0 2.8 %copy-start.1 = (f32[16,8192]{1,0:T(8,128)S(1)}, f32[16,8192]{1,0:T(8,128)}, u32[]{:S(2)}) copy-start(f32[16,8192]{1,0:T(8,128)} %get-tuple-element.11) | copy-start | bytes 1572868
  173.0 3.6 %copy-start.2 = (f32[16,1024]{1,0:T(8,128)S(1)}, f32[16,1024]{1,0:T(8,128)}, u32[]{:S(2)}) copy-start(f32[16,1024]{1,0:T(8,128)} %get-tuple-element.22) | copy-start | bytes 196612
  173.1 4.2 %copy-start = (f32[16,8192]{1,0:T(8,128)S(1)}, f32[16,8192]{1,0:T(8,128)}, u32[]{:S(2)}) copy-start(f32[16,8192]{1,0:T(8,128)} %get-tuple-element.13) | copy-start | bytes 1572868
  175.9 2.2 %copy-start.3 = (f32[16,128]{1,0:T(8,128)S(1)}, f32[16,128]{1,0:T(8,128)}, u32[]{:S(2)}) copy-start(f32[16,128]{1,0:T(8,128)} %get-tuple-element.24) | copy-start | bytes 24580

commit v5 on v4

--- a/solution.py
+++ b/solution.py
@@ -12,7 +12,7 @@
 HD = 128
 QUERY_PER_KV = 8
 RANK = 16
-QB = 256
+QB = 384
 
 EPSILON = 1e-05
 ADAPTER_SCALE = 2.0
@@ -83,7 +83,11 @@
 
 CHIPS = 64
 PLANE = 16
-LAG = 2
+LAG = 4
+AROUND = sorted(
+    ((a, b) for a in range(4) for b in range(4)),
+    key=lambda step: -sum(min(n, 4 - n) for n in step),
+)
 
 
 def step_kernel(
@@ -101,8 +105,7 @@
     out_hbm,
     ga_q_hbm,
     ga_v_hbm,
-    gb_q_hbm,
-    gb_v_hbm,
+    gb_hbm,
     raw,
     scale_scr,
     x_buf,
@@ -122,7 +125,7 @@
     down_b,
     down_t,
     dv_scr,
-    dq_scr,
+    dq_all,
     mid_scr,
     mid_recv,
     mid_all,
@@ -208,21 +211,21 @@
     own_copy.start()
 
     plane = lax.div(me.dp, 2) * 8 + me.fs
-    chip = plane * 4 + me.y
-
-    def of_chip(index):
-        at = lax.div(index, 4)
-        return (lax.div(at, 8) * 2 + me.core, lax.rem(at, 8), lax.rem(index, 4))
 
     barrier = pltpu.get_barrier_semaphore()
 
-    @pl.loop(1, CHIPS)
-    def _(o):
-        pl.semaphore_signal(
-            barrier, inc=1, device_id=of_chip(lax.rem(chip + o, CHIPS)), device_id_type=MESH
-        )
-
-    pl.semaphore_signal(barrier, inc=1, device_id=me.partner(), device_id_type=MESH)
+    neighbours = (
+        me.along(1),
+        me.along(3),
+        me.along(2),
+        me.near(1, 0),
+        me.near(3, 0),
+        me.near(0, 1),
+        me.near(0, 3),
+        me.partner(),
+    )
+    for device in neighbours:
+        pl.semaphore_signal(barrier, inc=1, device_id=device, device_id_type=MESH)
     for load in loads:
         load.start()
 
@@ -366,7 +369,7 @@
     loads[0].wait()
     normalize_chunk(0)
     normalize_chunk(middle)
-    pl.semaphore_wait(barrier, CHIPS)
+    pl.semaphore_wait(barrier, len(neighbours))
 
     w_start(0, 0, me.near(1, 0), 4, 0, source=w_hbm)
     w_start(0, 0, me.near(3, 0), 4, 1, source=w_hbm)
@@ -388,7 +391,6 @@
     down_scr[...] = jnp.zeros_like(down_scr)
 
     dv_scr[...] = jnp.zeros_like(dv_scr)
-    mid_scr[...] = jnp.zeros_like(mid_scr)
     up_part[...] = jnp.zeros_like(up_part)
     for load in loads[1:]:
         load.wait()
@@ -522,6 +524,7 @@
         own_grad(head).wait()
         for c in (1, 3, 2):
             grad_arrival(head, c).wait_recv()
+        head_lanes = pl.ds(pl.multiple_of(head * HD, HD), HD)
 
         for i in range(blocks):
             own_rows = slice(i * QB, (i + 1) * QB)
@@ -557,7 +560,7 @@
                 jnp.add, [dot_nn(ds[j], k_scr[j * QB : (j + 1) * QB, :]) for j in range(i + 1)]
             )
             dq = (dq * SCORE_SCALE).astype(jnp.bfloat16).astype(jnp.float32)
-            dq_scr[own_rows, :] = rotate(dq, cos_ref[own_rows, :], -sin_ref[own_rows, :]).astype(
+            dq_all[own_rows, head_lanes] = rotate(dq, cos_ref[own_rows, :], -sin_ref[own_rows, :]).astype(
                 jnp.bfloat16
             )
 
@@ -566,19 +569,11 @@
         def _():
             send_out(head - LAG)
 
-        up = dot_nn(down_t[:RANK, :], dq_scr[...])
-        up_part[0, head, :, :HD] = up[:8]
-        up_part[1, head, :, :HD] = up[8:]
-        lanes = pl.ds(pl.multiple_of(head * HD, HD), HD)
-        for b in range(4):
-            mid_scr[b, :RANK, :] += dot_nt(qup_ref[:, lanes], dq_scr[b * rows : (b + 1) * rows, :])
-
     dv = dv_scr[...].T.astype(jnp.bfloat16)
+    mid = jnp.concatenate([dot_nt(dq_all[...], qup_ref[...]), dot_nt(dv, vup_ref[...])], 1)
+    mid_t = mid.T
     for b in range(4):
-        mid_scr[b, RANK:, :] = dot_nt(vup_ref[...], dv[b * rows : (b + 1) * rows])
-    up = dot_nn(down_t[RANK:, :], dv)
-    up_part[0, heads, :, :HD] = up[:8]
-    up_part[1, heads, :, :HD] = up[8:]
+        mid_scr[b] = mid_t[:, b * rows : (b + 1) * rows]
 
     def mid_copy(c):
         return remote(
@@ -600,6 +595,14 @@
 
     for c in (1, 3, 2):
         mid_copy(c).start()
+    for n in range(4):
+        up = dot_nn(down_t[:RANK, :], dq_all[:, n * 256 : (n + 1) * 256])
+        for h in range(2):
+            up_part[0, 2 * n + h] = up[:8, h * HD : (h + 1) * HD]
+            up_part[1, 2 * n + h] = up[8:, h * HD : (h + 1) * HD]
+    up = dot_nn(down_t[RANK:, :], dv)
+    up_part[0, heads] = up[:8]
+    up_part[1, heads] = up[8:]
     for c in (1, 3, 2):
         mid_copy(c).wait_recv()
     mid_all[me.y] = (mid_scr[me.y] + mid_recv[0] + mid_recv[1] + mid_recv[2]).astype(jnp.bfloat16)
@@ -617,9 +620,9 @@
         made = dot_nn(mid_all[0], x_buf[0, 2 * me.y + half])
         for b in range(1, 4):
             made += dot_nn(mid_all[b], x_buf[b, 2 * me.y + half])
-        for r in range(4):
-            for k in range(4):
-                part[half, r * 4 + k] = made[r * 8 : (r + 1) * 8, k * 256 : (k + 1) * 256]
+        for r in range(2):
+            for k in range(8):
+                part[half, r * 8 + k] = made[r * 16 : (r + 1) * 16, k * HD : (k + 1) * HD]
 
     partial(1 - me.core)
     swap = remote(part.at[1 - me.core], part_recv, c_send.at[0], c_recv.at[0], me.partner())
@@ -629,14 +632,17 @@
     partial(me.core)
     up_swap.wait_recv()
     swap.wait_recv()
-    total[:, :, :256] = part[me.core] + part_recv[...]
-    total[:, :, 256:] = up_part[me.core] + up_recv[...]
-
-    @pl.loop(1, PLANE)
-    def _(o):
-        to = lax.rem(plane + o, PLANE)
+    total[:, :16] = part[me.core] + part_recv[...]
+    total[:, 16:] = up_part[me.core] + up_recv[...]
+
+    for n, (a, b) in enumerate(AROUND[:-1]):
+        dp, fs = me.plane(me.core, a, b)
         remote(
-            total.at[to], rs_recv.at[o - 1], r_send.at[0], r_recv.at[0], of_chip(to * 4 + me.y)
+            total.at[lax.div(dp, 2) * 8 + fs],
+            rs_recv.at[n],
+            r_send.at[0],
+            r_recv.at[0],
+            (dp, fs, me.y),
         ).start()
 
     many = remote(rs_recv, rs_recv, r_send.at[0], r_recv.at[0], me.partner())
@@ -644,40 +650,33 @@
     summed = total[plane]
     for o in range(PLANE - 1):
         summed += rs_recv[o]
-    summed = ADAPTER_SCALE * summed
-    final[...] = summed[:, :256]
-    up_final[...] = summed[:, 256:]
-
-    at_rows = pl.ds(pl.multiple_of(lax.div(plane, 4) * 8, 8), 8)
-    at_cols = pl.ds(pl.multiple_of(lax.rem(plane, 4) * 256, 256), 256)
+    final[...] = (ADAPTER_SCALE * summed[:16]).astype(jnp.bfloat16)
+    up_final[...] = summed[16:]
+
+    at_rows = pl.ds(pl.multiple_of(lax.div(plane, 8) * 16, 16), 16)
+    at_cols = pl.ds(pl.multiple_of(lax.rem(plane, 8) * HD, HD), HD)
     up_cols = pl.ds(pl.multiple_of(plane * HD, HD), HD)
 
-    @pl.loop(1, CHIPS)
-    def _(o):
-        to = lax.rem(chip + o, CHIPS)
+    for a, b in AROUND:
+        near = me.plane(me.core, a, b)
+        for c in (2, 1, 3, 0):
+            if a or b or c:
+                remote(
+                    final,
+                    res.at[me.core, me.y, at_rows, at_cols],
+                    r_send.at[1],
+                    r_recv.at[1],
+                    (*near, lax.rem(me.y + c, 4)),
+                ).start()
+    for a, b in AROUND[:-1]:
         remote(
-            final,
-            res.at[me.core, me.y, at_rows, at_cols],
-            r_send.at[1],
-            r_recv.at[1],
-            of_chip(to),
-        ).start()
-
-    @pl.loop(1, PLANE)
-    def _(o):
-        to = lax.rem(plane + o, PLANE)
-        remote(
-            up_final,
-            up_res.at[me.core, :, up_cols],
-            r_send.at[2],
-            r_recv.at[2],
-            of_chip(to * 4 + me.y),
+            up_final, up_res.at[me.core, :, up_cols], r_send.at[2], r_recv.at[2], me.near(a, b)
         ).start()
 
     res[me.core, me.y, at_rows, at_cols] = final[...]
     up_res[me.core, :, up_cols] = up_final[...]
     all_of = remote(ag_size, ag_size, r_send.at[1], r_recv.at[1], me.partner())
-    up_size = part_recv.at[pl.ds(0, PLANE - 1), :, pl.ds(0, HD)]
+    up_size = rs_recv.at[:, pl.ds(0, 8)]
     up_all = remote(up_size, up_size, r_send.at[2], r_recv.at[2], me.partner())
     up_all.wait_recv()
     up_half = remote(
@@ -706,11 +705,8 @@
         eight = pl.ds(pl.multiple_of(b * 8, 8), 8)
         return [
             pltpu.make_async_copy(
-                up_res.at[b, :, pl.ds(0, group)], gb_q_hbm.at[eight], write_sem.at[first]
-            ),
-            pltpu.make_async_copy(
-                up_res.at[b, :, pl.ds(group, HD)], gb_v_hbm.at[eight], write_sem.at[first + 1]
-            ),
+                up_res.at[b, :, pl.ds(0, group + HD)], gb_hbm.at[eight], write_sem.at[first]
+            )
         ]
 
     writes = grad_a_writes(me.core, 0) + grad_b_writes(me.core, 8)
@@ -754,13 +750,12 @@
     return pl.pallas_call(
         functools.partial(step_kernel, rows),
         in_specs=[anywhere] * 10,
-        out_specs=[anywhere] * 5,
+        out_specs=[anywhere] * 4,
         out_shape=[
             jax.ShapeDtypeStruct((rows, 4 * heads * HD), bf16),
-            jax.ShapeDtypeStruct((RANK, width), f32),
-            jax.ShapeDtypeStruct((RANK, width), f32),
-            jax.ShapeDtypeStruct((RANK, heads * HD), f32),
-            jax.ShapeDtypeStruct((RANK, HD), f32),
+            jax.ShapeDtypeStruct((RANK, width), bf16),
+            jax.ShapeDtypeStruct((RANK, width), bf16),
+            jax.ShapeDtypeStruct((RANK, (heads + 1) * HD), f32),
         ],
         scratch_shapes=[
             pltpu.VMEM((rows, width), bf16),
@@ -782,23 +777,23 @@
             pltpu.VMEM((seq, 2 * RANK), bf16),
             pltpu.VMEM((2 * RANK, seq), bf16),
             pltpu.VMEM((HD, seq), f32),
-            pltpu.VMEM((seq, HD), bf16),
+            pltpu.VMEM((seq, heads * HD), bf16),
             pltpu.VMEM((4, 2 * RANK, rows), f32),
             pltpu.VMEM((3, 2 * RANK, rows), f32),
             pltpu.VMEM((4, 2 * RANK, rows), bf16),
             pltpu.VMEM((heads, seq, HD), bf16),
             pltpu.VMEM((heads, seq, HD), bf16),
-            pltpu.VMEM((2, PLANE, 8, 256), f32),
-            pltpu.VMEM((PLANE, 8, 256), f32),
+            pltpu.VMEM((2, PLANE, 16, HD), f32),
+            pltpu.VMEM((PLANE, 16, HD), f32),
             pltpu.VMEM((2, PLANE, 8, HD), f32),
             pltpu.VMEM((PLANE, 8, HD), f32),
-            pltpu.VMEM((PLANE, 8, 256 + HD), f32),
-            pltpu.VMEM((PLANE - 1, 8, 256 + HD), f32),
-            pltpu.VMEM((8, 256), f32),
+            pltpu.VMEM((PLANE, 24, HD), f32),
+            pltpu.VMEM((PLANE - 1, 24, HD), f32),
+            pltpu.VMEM((16, HD), bf16),
             pltpu.VMEM((8, HD), f32),
-            pltpu.VMEM((2, 4, 2 * RANK, 1024), f32),
+            pltpu.VMEM((2, 4, 2 * RANK, 1024), bf16),
             pltpu.VMEM((2, 8, PLANE * HD), f32),
-            pltpu.VMEM((CHIPS - 1, 8, 256), f32),
+            pltpu.VMEM((CHIPS - 1, 16, HD), bf16),
             dma((4,)),
             dma((8,)),
             dma(()),
@@ -836,7 +831,7 @@
 
 def local(tokens, norm_gain, w_qkv, a_query, query_up_adapter, a_value, value_up_adapter, out_grad):
     cos, sin = rotary_tables(4 * tokens.shape[1])
-    out_rows, ga_query, ga_value, gb_query, gb_value = fused_step(
+    out_rows, ga_query, ga_value, grad_b = fused_step(
         tokens[0],
         norm_gain,
         w_qkv,
@@ -848,7 +843,13 @@
         sin,
         out_grad[0],
     )
-    return out_rows[None], ga_query.T, gb_query, ga_value.T, gb_value
+    return (
+        out_rows[None],
+        ga_query.T.astype(jnp.float32),
+        ADAPTER_SCALE * grad_b[:, : query_up_adapter.shape[1]],
+        ga_value.T.astype(jnp.float32),
+        ADAPTER_SCALE * grad_b[:, query_up_adapter.shape[1] :],
+    )
 
 
 def solution(mesh):

time: 179 us -> 169 us (0.944)
  Pallas kernels: 172 us -> 162 us
  other arithmetic: 0 us -> 4.95 us
  local copies, waits for them, and re-layouts: 5.62 us -> 1.15 us
    pallas_call x1, Pallas kernels: 172 us -> 162 us  [fused_step(): pl.pallas_call(functools.partial(step_kernel, rows), in_specs=[anywhere]...]
    unnamed x13 -> x3, local copies, waits for them, and re-layouts: 5.62 us -> 1.15 us
    mul x0 -> x2, other arithmetic: none -> 2.89 us  [the longest x1 1.47 us: local(): ADAPTER_SCALE * grad_b[:, :query_up_adapter.shape[1]]]
    convert_element_type x0 -> x1, other arithmetic: none -> 2.06 us  [local(): ga_value.T.astype(jnp.float32)]
where the time goes in v5:
time: 169 us
  Pallas kernels  162 us (96%)
  other arithmetic  4.95 us (3%)
    pallas_call x1, Pallas kernels, fused_step(): pl.pallas_call(functools.partial(step_kernel, rows), in_specs=[anywhere]...  162 us

profile of v5, /device:TPU:1, one launch (start us, length us, event | category | flops | bytes accessed | tf_op | source)
XLA Modules:
  0.0 168.6 jit_solution(16043782481223682509)
XLA Ops:
  0.6 161.9 %fused_step.1 = (bf16[192,4096]{1,0:T(8,128)(2,1)}, bf16[16,8192]{1,0:T(8,128)(2,1)}, bf16[16,8192]{1,0:T(8,128)(2,1)}, f32[16,1152]{1,0:T(8,128)}) custom-call(bf16[192,8192]{1,0:T(8,128)(2,1)} %bitcast.11, f32[1,8192]{1,0:T(1,128)} %bitcast.15, bf16[256,1280]{1,0:T(8,128)(2,1)} %w_hbm.1, bf16[16,8192]{1,0:T(8,128)(2,1)} %bitcast.13, ...), custom_call_target="tpu_custom_call" | custom-call | flops 16106127360 | bytes 10000000 | tf_op jit(solution)/shard_map/fused_step/pallas_call | solution.py:750
  162.5 0.0 copy-start
  162.5 1.4 slice_multiply_fusion.1
  163.9 1.5 slice_multiply_fusion
  165.4 2.1 %convert_bitcast_fusion = (f32[8192,16]{0,1:T(8,128)}, f32[8192,16]{0,1:T(8,128)}) fusion(bf16[16,8192]{1,0:T(8,128)(2,1)} %get-tuple-element.12, bf16[16,8192]{1,0:T(8,128)(2,1)} %get-tuple-element.10), kind=kLoop, calls=%fused_computation | loop fusion | flops 262144 | bytes 1572864 | tf_op jit(solution)/shard_map/convert_element_type | solution.py:850
  167.5 0.0 copy-done
  167.5 1.1 copy.16
Async XLA Ops:
  162.5 5.0 %copy-start = (bf16[192,4096]{1,0:T(8,128)(2,1)S(1)}, bf16[192,4096]{1,0:T(8,128)(2,1)}, u32[]{:S(2)}) copy-start(bf16[192,4096]{1,0:T(8,128)(2,1)} %get-tuple-element.9) | copy-start | bytes 4718596

commit v6 on v5

--- a/solution.py
+++ b/solution.py
@@ -45,7 +45,7 @@
 
 
 MESH = pl.DeviceIdType.MESH
-CHUNKS = 8
+CHUNKS = 16
 OFFSETS = (0, 3, 1, 2)
 
 
@@ -84,6 +84,7 @@
 CHIPS = 64
 PLANE = 16
 LAG = 4
+EARLY = 2
 AROUND = sorted(
     ((a, b) for a in range(4) for b in range(4)),
     key=lambda step: -sum(min(n, 4 - n) for n in step),
@@ -441,11 +442,17 @@
         x_copy(plus, c + middle, me.along(1), 1).wait_recv()
         x_start(plus, c + middle, me.along(3), 2)
 
+    def send_grads(first, last):
+        @pl.loop(first, last)
+        def _(h):
+            for c in (1, 3, 2):
+                grad_copy(h, c).start()
+
     @pl.loop(0, heads)
     def _(h):
         own_grad(h).start()
-        for c in (1, 3, 2):
-            grad_copy(h, c).start()
+
+    send_grads(0, EARLY)
 
     for event, (a, b) in enumerate(order):
         d_copy(1 - me.core, event, a, b).wait_recv()
@@ -506,6 +513,7 @@
         x_copy(far, c + middle, me.along(1), 2).wait_recv()
         multiply(far, c + middle)
 
+    send_grads(EARLY, heads)
     prepare(far)
     down_t[...] = down_b[...].astype(jnp.float32).T.astype(jnp.bfloat16)
 
@@ -609,20 +617,21 @@
     for c in (1, 3, 2):
         mid_share(c).start()
 
-    @pl.loop(heads - LAG, heads)
-    def _(h):
-        send_out(h)
-
+    send_out(4)
     for c in (1, 3, 2):
         mid_other(c).wait_recv()
 
     def partial(half):
-        made = dot_nn(mid_all[0], x_buf[0, 2 * me.y + half])
-        for b in range(1, 4):
-            made += dot_nn(mid_all[b], x_buf[b, 2 * me.y + half])
-        for r in range(2):
-            for k in range(8):
-                part[half, r * 8 + k] = made[r * 16 : (r + 1) * 16, k * HD : (k + 1) * HD]
+        for n in range(2):
+            chunk = 4 * me.y + 2 * half + n
+            made = dot_nn(mid_all[0], x_buf[0, chunk])
+            for b in range(1, 4):
+                made += dot_nn(mid_all[b], x_buf[b, chunk])
+            for r in range(2):
+                for k in range(4):
+                    part[half, r * 8 + n * 4 + k] = made[
+                        r * 16 : (r + 1) * 16, k * HD : (k + 1) * HD
+                    ]
 
     partial(1 - me.core)
     swap = remote(part.at[1 - me.core], part_recv, c_send.at[0], c_recv.at[0], me.partner())
@@ -645,13 +654,15 @@
             (dp, fs, me.y),
         ).start()
 
+    send_out(5)
+    send_out(6)
     many = remote(rs_recv, rs_recv, r_send.at[0], r_recv.at[0], me.partner())
     many.wait_recv()
     summed = total[plane]
     for o in range(PLANE - 1):
         summed += rs_recv[o]
     final[...] = (ADAPTER_SCALE * summed[:16]).astype(jnp.bfloat16)
-    up_final[...] = summed[16:]
+    up_final[...] = ADAPTER_SCALE * summed[16:]
 
     at_rows = pl.ds(pl.multiple_of(lax.div(plane, 8) * 16, 16), 16)
     at_cols = pl.ds(pl.multiple_of(lax.rem(plane, 8) * HD, HD), HD)
@@ -673,6 +684,7 @@
             up_final, up_res.at[me.core, :, up_cols], r_send.at[2], r_recv.at[2], me.near(a, b)
         ).start()
 
+    send_out(7)
     res[me.core, me.y, at_rows, at_cols] = final[...]
     up_res[me.core, :, up_cols] = up_final[...]
     all_of = remote(ag_size, ag_size, r_send.at[1], r_recv.at[1], me.partner())
@@ -829,6 +841,76 @@
     )(tokens, gain.reshape(1, width), w_qkv, aq_t, av_t, qup, vup, cos, sin, out_grad)
 
 
+def finish_kernel(
+    out_in, gq_in, gv_in, gb_in, out, gq, gv, bq, bv, rows, aq, av, fq, fv, b_buf, in_sem, out_sem
+):
+    parts = 4
+    size = rows.shape[0] // parts
+    cols = bq.shape[1]
+    small = [
+        pltpu.make_async_copy(src, dst, in_sem.at[parts + i])
+        for i, (src, dst) in enumerate(((gq_in, aq), (gv_in, av), (gb_in, b_buf)))
+    ]
+    large = [
+        pltpu.make_async_copy(
+            out_in.at[pl.ds(i * size, size)], rows.at[pl.ds(i * size, size)], in_sem.at[i]
+        )
+        for i in range(parts)
+    ]
+    for copy in small + large:
+        copy.start()
+    writes = []
+
+    def write(src, dst):
+        copy = pltpu.make_async_copy(src, dst, out_sem.at[len(writes)])
+        copy.start()
+        writes.append(copy)
+
+    small[0].wait()
+    fq[...] = aq[...].astype(jnp.float32)
+    write(fq, gq)
+    small[1].wait()
+    fv[...] = av[...].astype(jnp.float32)
+    write(fv, gv)
+    for i in range(parts):
+        large[i].wait()
+        write(rows.at[pl.ds(i * size, size)], out.at[pl.ds(i * size, size)])
+    small[2].wait()
+    write(b_buf.at[:, pl.ds(0, cols)], bq)
+    write(b_buf.at[:, pl.ds(cols, HD)], bv)
+    for copy in writes:
+        copy.wait()
+
+
+def finish(out_rows, ga_query, ga_value, grad_b):
+    anywhere = pl.BlockSpec(memory_space=pl.ANY)
+    cols = grad_b.shape[1] - HD
+    f32 = jnp.float32
+    return pl.pallas_call(
+        finish_kernel,
+        in_specs=[anywhere] * 4,
+        out_specs=[anywhere] * 5,
+        out_shape=[
+            jax.ShapeDtypeStruct(out_rows.shape, out_rows.dtype),
+            jax.ShapeDtypeStruct(ga_query.shape, f32),
+            jax.ShapeDtypeStruct(ga_value.shape, f32),
+            jax.ShapeDtypeStruct((RANK, cols), f32),
+            jax.ShapeDtypeStruct((RANK, HD), f32),
+        ],
+        scratch_shapes=[
+            pltpu.VMEM(out_rows.shape, out_rows.dtype),
+            pltpu.VMEM(ga_query.shape, ga_query.dtype),
+            pltpu.VMEM(ga_value.shape, ga_value.dtype),
+            pltpu.VMEM(ga_query.shape, f32),
+            pltpu.VMEM(ga_value.shape, f32),
+            pltpu.VMEM(grad_b.shape, f32),
+            pltpu.SemaphoreType.DMA((7,)),
+            pltpu.SemaphoreType.DMA((8,)),
+        ],
+        name="finish",
+    )(out_rows, ga_query, ga_value, grad_b)
+
+
 def local(tokens, norm_gain, w_qkv, a_query, query_up_adapter, a_value, value_up_adapter, out_grad):
     cos, sin = rotary_tables(4 * tokens.shape[1])
     out_rows, ga_query, ga_value, grad_b = fused_step(
@@ -843,13 +925,8 @@
         sin,
         out_grad[0],
     )
-    return (
-        out_rows[None],
-        ga_query.T.astype(jnp.float32),
-        ADAPTER_SCALE * grad_b[:, : query_up_adapter.shape[1]],
-        ga_value.T.astype(jnp.float32),
-        ADAPTER_SCALE * grad_b[:, query_up_adapter.shape[1] :],
-    )
+    out_rows, ga_query, ga_value, gb_query, gb_value = finish(out_rows, ga_query, ga_value, grad_b)
+    return out_rows[None], ga_query.T, gb_query, ga_value.T, gb_value
 
 
 def solution(mesh):

time: 169 us -> 165 us (0.976)
  other arithmetic: 4.95 us -> 0 us
  Pallas kernels: 162 us -> 164 us
    mul x2 -> x0, other arithmetic: 2.89 us -> none  [the longest x1 1.47 us: local(): ADAPTER_SCALE * grad_b[:, :query_up_adapter.shape[1]]]
    pallas_call x0 -> x1, Pallas kernels: none -> 2.61 us  [finish(): pl.pallas_call(finish_kernel, in_specs=[anywhere] * 4, out_specs=[anywher...]
    convert_element_type x1 -> x0, other arithmetic: 2.06 us -> none  [local(): ga_value.T.astype(jnp.float32)]
where the time goes in v6:
time: 165 us
  Pallas kernels  164 us (99%)
    pallas_call x1, Pallas kernels, fused_step(): pl.pallas_call(functools.partial(step_kernel, rows), in_specs=[anywhere]...  162 us

profile of v6, /device:TPU:1, one launch (start us, length us, event | category | flops | bytes accessed | tf_op | source)
XLA Modules:
  0.0 165.0 jit_solution(8412266425500506182)
XLA Ops:
  0.6 161.7 %fused_step.1 = (bf16[192,4096]{1,0:T(8,128)(2,1)}, bf16[16,8192]{1,0:T(8,128)(2,1)}, bf16[16,8192]{1,0:T(8,128)(2,1)}, f32[16,1152]{1,0:T(8,128)}) custom-call(bf16[192,8192]{1,0:T(8,128)(2,1)} %bitcast.8, f32[1,8192]{1,0:T(1,128)} %bitcast.15, bf16[256,1280]{1,0:T(8,128)(2,1)} %w_hbm.1, bf16[16,8192]{1,0:T(8,128)(2,1)} %bitcast.13, ...), custom_call_target="tpu_custom_call" | custom-call | flops 16106127360 | bytes 10000000 | tf_op jit(solution)/shard_map/fused_step/pallas_call | solution.py:762
  162.4 2.6 %finish.1 = (bf16[192,4096]{1,0:T(8,128)(2,1)}, f32[16,8192]{1,0:T(8,128)}, f32[16,8192]{1,0:T(8,128)}, f32[16,1024]{1,0:T(8,128)}, f32[16,128]{1,0:T(8,128)}) custom-call(bf16[192,4096]{1,0:T(8,128)(2,1)} %get-tuple-element.14.out_in, bf16[16,8192]{1,0:T(8,128)(2,1)} %get-tuple-element.15.gq_in, bf16[16,8192]{1,0:T(8,128)(2,1)} %get-tuple-element.16.gv_in, ...), custom_call_target="tpu_custom_call" | custom-call | tf_op jit(solution)/shard_map/finish/pallas_call | solution.py:889

commit v7 on v6

--- a/solution.py
+++ b/solution.py
@@ -128,6 +128,7 @@
     dv_scr,
     dq_all,
     mid_scr,
+    mid_mine,
     mid_recv,
     mid_all,
     g_buf,
@@ -577,29 +578,20 @@
         def _():
             send_out(head - LAG)
 
-    dv = dv_scr[...].T.astype(jnp.bfloat16)
-    mid = jnp.concatenate([dot_nt(dq_all[...], qup_ref[...]), dot_nt(dv, vup_ref[...])], 1)
-    mid_t = mid.T
+    dv_t = dv_scr[...].astype(jnp.bfloat16)
+    mid_q = dot_nt(dq_all[...], qup_ref[...]).T
+    mid_v = dot_nn(vup_ref[...], dv_t)
     for b in range(4):
-        mid_scr[b] = mid_t[:, b * rows : (b + 1) * rows]
+        lanes = slice(b * rows, (b + 1) * rows)
+        mid_scr[b, :RANK] = mid_q[:, lanes]
+        mid_scr[b, RANK:] = mid_v[:, lanes]
+        mid_mine[b, :RANK] = mid_q[:, lanes].astype(jnp.bfloat16)
+        mid_mine[b, RANK:] = mid_v[:, lanes].astype(jnp.bfloat16)
 
     def mid_copy(c):
         return remote(
-            mid_scr.at[lax.rem(me.y + c, 4)],
-            mid_recv.at[c - 1],
-            m_send.at[c - 1],
-            m_recv.at[c - 1],
-            me.along(c),
-        )
-
-    def mid_share(c):
-        return remote(
-            mid_all.at[me.y], mid_all.at[me.y], m_send.at[2 + c], m_recv.at[2 + c], me.along(c)
-        )
-
-    def mid_other(c):
-        ref = mid_all.at[lax.rem(me.y + 4 - c, 4)]
-        return remote(ref, ref, m_send.at[2 + c], m_recv.at[2 + c], me.along(c))
+            mid_mine, mid_recv.at[c - 1], m_send.at[c - 1], m_recv.at[c - 1], me.along(c)
+        )
 
     for c in (1, 3, 2):
         mid_copy(c).start()
@@ -608,18 +600,17 @@
         for h in range(2):
             up_part[0, 2 * n + h] = up[:8, h * HD : (h + 1) * HD]
             up_part[1, 2 * n + h] = up[8:, h * HD : (h + 1) * HD]
-    up = dot_nn(down_t[RANK:, :], dv)
+    up = dot_nt(down_t[RANK:, :], dv_t)
     up_part[0, heads] = up[:8]
     up_part[1, heads] = up[8:]
     for c in (1, 3, 2):
         mid_copy(c).wait_recv()
-    mid_all[me.y] = (mid_scr[me.y] + mid_recv[0] + mid_recv[1] + mid_recv[2]).astype(jnp.bfloat16)
-    for c in (1, 3, 2):
-        mid_share(c).start()
-
     send_out(4)
-    for c in (1, 3, 2):
-        mid_other(c).wait_recv()
+    for b in range(4):
+        summed = mid_scr[b]
+        for c in range(3):
+            summed += mid_recv[c, b].astype(jnp.float32)
+        mid_all[b] = summed.astype(jnp.bfloat16)
 
     def partial(half):
         for n in range(2):
@@ -641,8 +632,8 @@
     partial(me.core)
     up_swap.wait_recv()
     swap.wait_recv()
-    total[:, :16] = part[me.core] + part_recv[...]
-    total[:, 16:] = up_part[me.core] + up_recv[...]
+    total[:, :16] = (part[me.core] + part_recv[...]).astype(jnp.bfloat16)
+    total[:, 16:] = (up_part[me.core] + up_recv[...]).astype(jnp.bfloat16)
 
     for n, (a, b) in enumerate(AROUND[:-1]):
         dp, fs = me.plane(me.core, a, b)
@@ -658,9 +649,9 @@
     send_out(6)
     many = remote(rs_recv, rs_recv, r_send.at[0], r_recv.at[0], me.partner())
     many.wait_recv()
-    summed = total[plane]
+    summed = total[plane].astype(jnp.float32)
     for o in range(PLANE - 1):
-        summed += rs_recv[o]
+        summed += rs_recv[o].astype(jnp.float32)
     final[...] = (ADAPTER_SCALE * summed[:16]).astype(jnp.bfloat16)
     up_final[...] = ADAPTER_SCALE * summed[16:]
 
@@ -688,7 +679,7 @@
     res[me.core, me.y, at_rows, at_cols] = final[...]
     up_res[me.core, :, up_cols] = up_final[...]
     all_of = remote(ag_size, ag_size, r_send.at[1], r_recv.at[1], me.partner())
-    up_size = rs_recv.at[:, pl.ds(0, 8)]
+    up_size = ag_size.at[pl.ds(0, PLANE - 1)]
     up_all = remote(up_size, up_size, r_send.at[2], r_recv.at[2], me.partner())
     up_all.wait_recv()
     up_half = remote(
@@ -743,7 +734,6 @@
         copy.start()
     for c in (1, 3, 2):
         mid_copy(c).wait_send()
-        mid_share(c).wait_send()
     for copy in (up_swap, swap, many, all_of, up_all, up_half, half):
         copy.wait_send()
     for copy in writes + late:
@@ -791,7 +781,8 @@
             pltpu.VMEM((HD, seq), f32),
             pltpu.VMEM((seq, heads * HD), bf16),
             pltpu.VMEM((4, 2 * RANK, rows), f32),
-            pltpu.VMEM((3, 2 * RANK, rows), f32),
+            pltpu.VMEM((4, 2 * RANK, rows), bf16),
+            pltpu.VMEM((3, 4, 2 * RANK, rows), bf16),
             pltpu.VMEM((4, 2 * RANK, rows), bf16),
             pltpu.VMEM((heads, seq, HD), bf16),
             pltpu.VMEM((heads, seq, HD), bf16),
@@ -799,8 +790,8 @@
             pltpu.VMEM((PLANE, 16, HD), f32),
             pltpu.VMEM((2, PLANE, 8, HD), f32),
             pltpu.VMEM((PLANE, 8, HD), f32),
-            pltpu.VMEM((PLANE, 24, HD), f32),
-            pltpu.VMEM((PLANE - 1, 24, HD), f32),
+            pltpu.VMEM((PLANE, 24, HD), bf16),
+            pltpu.VMEM((PLANE - 1, 24, HD), bf16),
             pltpu.VMEM((16, HD), bf16),
             pltpu.VMEM((8, HD), f32),
             pltpu.VMEM((2, 4, 2 * RANK, 1024), bf16),
@@ -821,8 +812,8 @@
             dma((heads, 3)),
             dma((heads, 3)),
             dma((heads, 3)),
-            dma((6,)),
-            dma((6,)),
+            dma((3,)),
+            dma((3,)),
             dma((4,)),
             dma((4,)),
             dma((3,)),

time: 165 us -> 162 us (0.982)
  Pallas kernels: 164 us -> 161 us
    pallas_call x1, Pallas kernels: 162 us -> 158 us  [fused_step(): pl.pallas_call(functools.partial(step_kernel, rows), in_specs=[anywhere]...]
where the time goes in v7:
time: 162 us; the launch traced here: 161 us
  Pallas kernels  161 us (99%)
    pallas_call x1, Pallas kernels, fused_step(): pl.pallas_call(functools.partial(step_kernel, rows), in_specs=[anywhere]...  158 us

profile of v7, /device:TPU:1, one launch (start us, length us, event | category | flops | bytes accessed | tf_op | source)
XLA Modules:
  0.0 161.5 jit_solution(14014687742235823757)
XLA Ops:
  0.6 158.2 %fused_step.1 = (bf16[192,4096]{1,0:T(8,128)(2,1)}, bf16[16,8192]{1,0:T(8,128)(2,1)}, bf16[16,8192]{1,0:T(8,128)(2,1)}, f32[16,1152]{1,0:T(8,128)}) custom-call(bf16[192,8192]{1,0:T(8,128)(2,1)} %bitcast.8, f32[1,8192]{1,0:T(1,128)} %bitcast.15, bf16[256,1280]{1,0:T(8,128)(2,1)} %w_hbm.1, bf16[16,8192]{1,0:T(8,128)(2,1)} %bitcast.13, ...), custom_call_target="tpu_custom_call" | custom-call | flops 16106127360 | bytes 10000000 | tf_op jit(solution)/shard_map/fused_step/pallas_call | solution.py:752
  158.9 2.6 %finish.1 = (bf16[192,4096]{1,0:T(8,128)(2,1)}, f32[16,8192]{1,0:T(8,128)}, f32[16,8192]{1,0:T(8,128)}, f32[16,1024]{1,0:T(8,128)}, f32[16,128]{1,0:T(8,128)}) custom-call(bf16[192,4096]{1,0:T(8,128)(2,1)} %get-tuple-element.14.out_in, bf16[16,8192]{1,0:T(8,128)(2,1)} %get-tuple-element.15.gq_in, bf16[16,8192]{1,0:T(8,128)(2,1)} %get-tuple-element.16.gv_in, ...), custom_call_target="tpu_custom_call" | custom-call | tf_op jit(solution)/shard_map/finish/pallas_call | solution.py:880

commit v8 on v7

--- a/solution.py
+++ b/solution.py
@@ -848,7 +848,7 @@
         )
         for i in range(parts)
     ]
-    for copy in small + large:
+    for copy in large + small:
         copy.start()
     writes = []
 
@@ -857,15 +857,15 @@
         copy.start()
         writes.append(copy)
 
+    for i in range(parts):
+        large[i].wait()
+        write(rows.at[pl.ds(i * size, size)], out.at[pl.ds(i * size, size)])
     small[0].wait()
     fq[...] = aq[...].astype(jnp.float32)
     write(fq, gq)
     small[1].wait()
     fv[...] = av[...].astype(jnp.float32)
     write(fv, gv)
-    for i in range(parts):
-        large[i].wait()
-        write(rows.at[pl.ds(i * size, size)], out.at[pl.ds(i * size, size)])
     small[2].wait()
     write(b_buf.at[:, pl.ds(0, cols)], bq)
     write(b_buf.at[:, pl.ds(cols, HD)], bv)

time: 162 us -> 162 us (level)
  no operation moved by 1% of the time
where the time goes in v8:
time: 162 us; the launch traced here: 161 us
  Pallas kernels  161 us (99%)
    pallas_call x1, Pallas kernels, fused_step(): pl.pallas_call(functools.partial(step_kernel, rows), in_specs=[anywhere]...  158 us

profile of v8, /device:TPU:1, one launch (start us, length us, event | category | flops | bytes accessed | tf_op | source)
XLA Modules:
  0.0 161.5 jit_solution(14115099177973556757)
XLA Ops:
  0.6 158.2 %fused_step.1 = (bf16[192,4096]{1,0:T(8,128)(2,1)}, bf16[16,8192]{1,0:T(8,128)(2,1)}, bf16[16,8192]{1,0:T(8,128)(2,1)}, f32[16,1152]{1,0:T(8,128)}) custom-call(bf16[192,8192]{1,0:T(8,128)(2,1)} %bitcast.8, f32[1,8192]{1,0:T(1,128)} %bitcast.15, bf16[256,1280]{1,0:T(8,128)(2,1)} %w_hbm.1, bf16[16,8192]{1,0:T(8,128)(2,1)} %bitcast.13, ...), custom_call_target="tpu_custom_call" | custom-call | flops 16106127360 | bytes 10000000 | tf_op jit(solution)/shard_map/fused_step/pallas_call | solution.py:752
  158.9 2.6 %finish.1 = (bf16[192,4096]{1,0:T(8,128)(2,1)}, f32[16,8192]{1,0:T(8,128)}, f32[16,8192]{1,0:T(8,128)}, f32[16,1024]{1,0:T(8,128)}, f32[16,128]{1,0:T(8,128)}) custom-call(bf16[192,4096]{1,0:T(8,128)(2,1)} %get-tuple-element.14.out_in, bf16[16,8192]{1,0:T(8,128)(2,1)} %get-tuple-element.15.gq_in, bf16[16,8192]{1,0:T(8,128)(2,1)} %get-tuple-element.16.gv_in, ...), custom_call_target="tpu_custom_call" | custom-call | tf_op jit(solution)/shard_map/finish/pallas_call | solution.py:880
